TPU v7x, 128 devices: a whole 4x4x4 slice. The times are simulated.
128 devices in a mesh: seq: 32 (over z_lo, y, x), grp: 4 (over z_hi, core).
Axes of the slice: x: 4, y: 4, z: 4 (z_hi: 2, z_lo: 2; z = z_hi * 2 + z_lo), core: 2. Of those that a mesh axis runs over, the one named last changes fastest.
Arguments:
- queries: bfloat16 [4, 8192, 1536], P('grp', 'seq'), may hold values from -6 to 6
- key_rows: bfloat16 [4, 8192, 1536], P('grp', 'seq'), may hold values from -6 to 6
- value_rows: bfloat16 [4, 8192, 1536], P('grp', 'seq'), may hold values from -6 to 6
- attn_cotangent: bfloat16 [4, 8192, 1536], P('grp', 'seq'), may hold values from -6 to 6
- mixer_input: bfloat16 [4, 4096, 3072], P('grp', 'seq'), may hold values from -6 to 6
- step_raw: bfloat16 [4, 4096, 3072], P('grp', 'seq'), may hold values from -3 to 3
- state_in: bfloat16 [4, 8, 4096], P('grp', None, 'seq'), may hold values from -6 to 6
- state_out: bfloat16 [4, 8, 4096], P('grp', None, 'seq'), may hold values from -6 to 6
- mixer_cotangent: bfloat16 [4, 4096, 3072], P('grp', 'seq'), may hold values from -0.3125 to 0.3125
- decay_log: float32 [8, 3072], replicated, may hold values from -9 to 0.5
- step_bias: float32 [3072], replicated, may hold values from -4 to -1
- skip_gain: float32 [3072], replicated, may hold values from 0.5 to 1.5
Outputs:
- grad_queries: bfloat16 [4, 8192, 1536], P('grp', 'seq')
- grad_keys: bfloat16 [4, 8192, 1536], P('grp', 'seq')
- grad_values: bfloat16 [4, 8192, 1536], P('grp', 'seq')
- grad_input: bfloat16 [4, 4096, 3072], P('grp', 'seq')
- grad_step: bfloat16 [4, 4096, 3072], P('grp', 'seq')
- grad_state_in: bfloat16 [4, 8, 4096], P('grp', None, 'seq')
- grad_state_out: bfloat16 [4, 8, 4096], P('grp', None, 'seq')
- grad_decay_log: float32 [8, 3072], replicated
- grad_step_bias: float32 [3072], replicated
- grad_skip_gain: float32 [3072], replicated
All inputs are finite; a program needn't handle non-finite values.
Results may differ from a plain program's by a relative error of at most 0.0097.
Values may be sent and summed in bfloat16 or wider, within the bound.
A program may use at most 128 MiB of HBM per device.

v0:
```python
from functools import partial

import jax
import jax.numpy as jnp
from jax import lax
from jax.sharding import Mesh
from jax.sharding import PartitionSpec as P

HEAD_DIM = 128
HEAD_GROUP = 1
BLOCK = 32
WINDOW = 1024
SEQ = ("seq_0", "seq_1", "seq_2")
SEQ_GRP = ("seq_0", "seq_1", "seq_2", "grp")


NEG_BIG = -1e30


def shifted(block, axis, distance):
    devices = range(lax.axis_size(axis))
    route = [(i - distance, i) for i in devices if i - distance in devices]
    return lax.ppermute(block, axis, route)


def neutral_like(shard, identity):
    return jax.tree.map(
        lambda part, zero: jnp.zeros_like(part) + jnp.asarray(zero, part.dtype), shard, identity
    )


def carried_in(shard, axes, combine, identity, reverse):
    before = start = neutral_like(shard, identity)
    subtotal = shard
    for axis in reversed(axes):
        size, position = (lax.axis_size(axis), lax.axis_index(axis))
        pieces = jax.tree.map(lambda part: lax.all_gather(part, axis), subtotal)
        inside, subtotal = (start, start)
        for k in reversed(range(size)) if reverse else range(size):
            passed = k > position if reverse else k < position
            subtotal = combine(subtotal, jax.tree.map(lambda part: part[k], pieces))
            inside = jax.tree.map(lambda new, old: jnp.where(passed, new, old), subtotal, inside)
        before = combine(inside, before)
    return before


def compose(earlier, later):
    return (earlier[0] * later[0], later[0] * earlier[1] + later[1])


def split_heads(array, groups):
    return jnp.moveaxis(array.reshape(array.shape[0], groups, -1), 1, 0)


def merge_heads(array):
    return jnp.moveaxis(array, 0, 1).reshape(array.shape[1], -1)


def to_heads(array):
    return array.reshape(array.shape[0], -1, HEAD_DIM)


def window_block(query_block, key_stack, value_stack, grad_block, first_valid):
    block_width = query_block.shape[0]
    stack_rows = key_stack.shape[0]
    lead = stack_rows - block_width
    score_scale = query_block.shape[2] ** (-0.5)
    scores = (
        jnp.einsum("qhd,khd->hqk", query_block, key_stack, preferred_element_type=jnp.float32)
        * score_scale
    )
    row_pos = jnp.arange(block_width)[:, None]
    col_pos = jnp.arange(stack_rows)[None, :]
    allowed = (
        (col_pos <= row_pos + lead) & (col_pos > row_pos + lead - WINDOW) & (col_pos >= first_valid)
    )
    scores = jnp.where(allowed[None], scores, NEG_BIG)
    row_max = jnp.max(scores, axis=2)
    raw_weights = jnp.exp(scores - row_max[:, :, None])
    row_sum = jnp.sum(raw_weights, axis=2)
    softmax_prob = raw_weights / row_sum[:, :, None]
    prob_half = softmax_prob.astype(jnp.bfloat16)
    output = jnp.einsum("hqk,khd->qhd", prob_half, value_stack, preferred_element_type=jnp.float32)
    row_delta = jnp.sum(output * grad_block.astype(jnp.float32), axis=2)
    grad_prob = jnp.einsum(
        "qhd,khd->hqk", grad_block, value_stack, preferred_element_type=jnp.float32
    )
    grad_score = (softmax_prob * (grad_prob - row_delta.T[:, :, None])).astype(jnp.bfloat16)
    grad_query = (
        jnp.einsum("hqk,khd->qhd", grad_score, key_stack, preferred_element_type=jnp.float32)
        * score_scale
    )
    grad_key = (
        jnp.einsum("hqk,qhd->khd", grad_score, query_block, preferred_element_type=jnp.float32)
        * score_scale
    )
    grad_value = jnp.einsum(
        "hqk,qhd->khd", prob_half, grad_block, preferred_element_type=jnp.float32
    )
    return (grad_query, grad_key, grad_value, row_max, row_sum, row_delta.T)


def attention_part(queries, key_rows, value_rows, attn_cotangent):
    query_local = queries[0]
    key_local = key_rows[0]
    value_local = value_rows[0]
    grad_local = attn_cotangent[0]
    block_width = query_local.shape[0]
    reach_blocks = (WINDOW + block_width - 1) // block_width
    groups = query_local.shape[1] // (HEAD_GROUP * HEAD_DIM)
    earlier_keys = []
    earlier_values = []
    for distance in range(reach_blocks, 0, -1):
        prev_keys, prev_values = shifted((key_local, value_local), SEQ, distance)
        earlier_keys.append(prev_keys)
        earlier_values.append(prev_values)
    key_stack = jnp.concatenate(earlier_keys + [key_local], 0)
    value_stack = jnp.concatenate(earlier_values + [value_local], 0)
    first_valid = jnp.maximum(reach_blocks - lax.axis_index(SEQ), 0) * block_width

    def per_group(pieces, own_only):
        results = window_block(
            to_heads(pieces[0]),
            to_heads(pieces[1]),
            to_heads(pieces[2]),
            to_heads(pieces[3]),
            first_valid,
        )
        flat_query = results[0].reshape(block_width, -1)
        flat_key = results[1].reshape(results[1].shape[0], -1)
        flat_value = results[2].reshape(results[2].shape[0], -1)
        return (flat_query, flat_key, flat_value, results[3], results[4], results[5])

    grouped = (
        split_heads(query_local, groups),
        split_heads(key_stack, groups),
        split_heads(value_stack, groups),
        split_heads(grad_local, groups),
    )
    grad_query, key_all, value_all, row_max, row_sum, row_delta = lax.map(
        partial(per_group, own_only=False), grouped
    )
    lead = reach_blocks * block_width
    grad_key = key_all[:, lead:]
    grad_value = value_all[:, lead:]
    for distance in range(1, reach_blocks + 1):
        begin = lead - distance * block_width
        back_key, back_value = (
            shifted(
                key_all[:, begin : begin + block_width].astype(jnp.bfloat16), SEQ, -distance
            ).astype(jnp.float32),
            shifted(
                value_all[:, begin : begin + block_width].astype(jnp.bfloat16), SEQ, -distance
            ).astype(jnp.float32),
        )
        grad_key = grad_key + back_key
        grad_value = grad_value + back_value
    return (
        merge_heads(grad_query).astype(jnp.bfloat16)[None],
        merge_heads(grad_key).astype(jnp.bfloat16)[None],
        merge_heads(grad_value).astype(jnp.bfloat16)[None],
    )


def mixer_part(
    mixer_input, step_raw, state_in, state_out, mixer_cotangent, decay_log, step_bias, skip_gain
):
    input_rows = mixer_input[0].astype(jnp.float32)
    raw_rows = step_raw[0].astype(jnp.float32) + step_bias
    step_rows = jax.nn.softplus(raw_rows)
    cot_rows = mixer_cotangent[0].astype(jnp.float32)
    in_proj = state_in[0].astype(jnp.float32).T
    out_proj = state_out[0].astype(jnp.float32).T
    decay_rate = -jnp.exp(decay_log)
    token_count = input_rows.shape[0]
    blocks = token_count // BLOCK
    inner = input_rows.shape[1]
    nstate = in_proj.shape[1]
    lower_ones = (jnp.arange(BLOCK)[:, None] >= jnp.arange(BLOCK)[None, :]).astype(jnp.float32)

    def by_block(array):
        return array.reshape(blocks, BLOCK, array.shape[1])

    def running_sum(table, array):
        flat = jnp.dot(table, array.reshape(BLOCK, -1), preferred_element_type=jnp.float32)
        return flat.reshape(array.shape)

    sliced = (
        by_block(input_rows),
        by_block(step_rows),
        by_block(cot_rows),
        by_block(in_proj),
        by_block(out_proj),
    )

    def local_totals(carry, item):
        state_sum, step_sum = carry
        input_blk, step_blk, cot_blk, in_blk, out_blk = item
        cumul = jnp.cumsum(step_blk, axis=0)
        block_total = cumul[-1]
        tail_decay = jnp.exp(decay_rate[None] * (block_total[None] - cumul)[:, None, :])
        drive = (step_blk * input_blk)[:, None, :] * in_blk[:, :, None]
        new_state = jnp.exp(decay_rate * block_total) * state_sum + jnp.sum(
            tail_decay * drive, axis=0
        )
        head_decay = jnp.exp(decay_rate[None] * (step_sum[None] + cumul)[:, None, :])
        source = cot_blk[:, None, :] * out_blk[:, :, None]
        back_part = jnp.sum(head_decay * source, axis=0)
        return ((new_state, step_sum + block_total), (state_sum, step_sum, back_part))

    zero_state = jnp.zeros((nstate, inner), jnp.float32)
    zero_chan = jnp.zeros((inner,), jnp.float32)
    (state_end, step_total), (local_starts, step_before, back_parts) = lax.scan(
        local_totals, (zero_state, zero_chan), sliced
    )
    back_total = jnp.sum(back_parts, axis=0)
    decay_all = jnp.exp(decay_rate * step_total)
    identity = (jnp.ones_like(zero_state), zero_state)
    state_carry = carried_in((decay_all, state_end), SEQ, compose, identity, False)[1]
    adjoint_carry = carried_in((decay_all, back_total), SEQ, compose, identity, True)[1]
    starts = local_starts + jnp.exp(decay_rate[None] * step_before[:, None, :]) * state_carry[None]

    def block_back(carry, item):
        adjoint_in, rate_acc = carry
        input_blk, step_blk, cot_blk, in_blk, out_blk, start = item
        cumul = jnp.cumsum(step_blk, axis=0)
        block_total = cumul[-1]
        centred = cumul - 0.5 * block_total[None]
        rise = jnp.exp(decay_rate[None] * centred[:, None, :])
        fall = jnp.exp(-decay_rate[None] * centred[:, None, :])
        decay = jnp.exp(step_blk[:, None, :] * decay_rate[None])
        drive = (step_blk * input_blk)[:, None, :] * in_blk[:, :, None]
        states = (
            rise * running_sum(lower_ones, fall * drive)
            + jnp.exp(decay_rate[None] * cumul[:, None, :]) * start[None]
        )
        prev_states = jnp.concatenate([start[None], states[:-1]], 0)
        source = cot_blk[:, None, :] * out_blk[:, :, None]
        tail = jnp.exp(decay_rate[None] * (block_total[None] - cumul)[:, None, :])
        adjoint = fall * running_sum(lower_ones.T, rise * source) + tail * adjoint_in[None]
        weighted = adjoint * prev_states * decay
        rate_acc = rate_acc + jnp.sum(weighted * step_blk[:, None, :], axis=0)
        adjoint_proj = jnp.sum(adjoint * in_blk[:, :, None], axis=1)
        grad_x = skip_gain * cot_blk + step_blk * adjoint_proj
        grad_dt = input_blk * adjoint_proj + jnp.sum(weighted * decay_rate[None], axis=1)
        grad_in = jnp.sum(adjoint * (step_blk * input_blk)[:, None, :], axis=2)
        grad_out = jnp.sum(cot_blk[:, None, :] * states, axis=2)
        return ((decay[0] * adjoint[0], rate_acc), (grad_x, grad_dt, grad_in, grad_out))

    (_, rate_grad), (grad_x, grad_dt, grad_in, grad_out) = lax.scan(
        block_back, (adjoint_carry, zero_state), sliced + (starts,), reverse=True
    )
    grad_x = grad_x.reshape(token_count, inner)
    grad_raw = grad_dt.reshape(token_count, inner) * jax.nn.sigmoid(raw_rows)
    grad_in = grad_in.reshape(token_count, nstate).T
    grad_out = grad_out.reshape(token_count, nstate).T
    summed = lax.psum(
        (rate_grad * decay_rate, jnp.sum(grad_raw, axis=0), jnp.sum(cot_rows * input_rows, axis=0)),
        SEQ_GRP,
    )
    return (
        grad_x.astype(jnp.bfloat16)[None],
        grad_raw.astype(jnp.bfloat16)[None],
        grad_in.astype(jnp.bfloat16)[None],
        grad_out.astype(jnp.bfloat16)[None],
        summed[0],
        summed[1],
        summed[2],
    )


def on_device(
    queries,
    key_rows,
    value_rows,
    attn_cotangent,
    mixer_input,
    step_raw,
    state_in,
    state_out,
    mixer_cotangent,
    decay_log,
    step_bias,
    skip_gain,
):
    grad_queries, grad_keys, grad_values = attention_part(
        queries, key_rows, value_rows, attn_cotangent
    )
    mixer_out = mixer_part(
        mixer_input, step_raw, state_in, state_out, mixer_cotangent, decay_log, step_bias, skip_gain
    )
    return (grad_queries, grad_keys, grad_values) + mixer_out


def solution(mesh):
    torus = Mesh(
        mesh.devices.reshape(2, 4, 4, mesh.shape["grp"]), ("seq_0", "seq_1", "seq_2", "grp")
    )
    in_specs = (
        P("grp", SEQ, None),
        P("grp", SEQ, None),
        P("grp", SEQ, None),
        P("grp", SEQ, None),
        P("grp", SEQ, None),
        P("grp", SEQ, None),
        P("grp", None, SEQ),
        P("grp", None, SEQ),
        P("grp", SEQ, None),
        P(),
        P(),
        P(),
    )
    out_specs = (
        P("grp", SEQ, None),
        P("grp", SEQ, None),
        P("grp", SEQ, None),
        P("grp", SEQ, None),
        P("grp", SEQ, None),
        P("grp", None, SEQ),
        P("grp", None, SEQ),
        P(),
        P(),
        P(),
    )
    return jax.shard_map(
        on_device, mesh=torus, in_specs=in_specs, out_specs=out_specs, check_vma=False
    )
```

profile of v0, /device:TPU:1, one launch (start us, length us, event | category | flops | bytes accessed | tf_op | source)
XLA Modules:
  0.0 782.0 jit_solution(8084962262362505843)
XLA Ops:
  9.7 4.9 collective-permute-start
  14.6 5.3 collective-permute-start.1
  40.5 25.5 %while.64 = (s32[]{:T(128)}, f32[8,3072]{1,0:T(8,128)S(1)}, f32[3072]{0:T(1024)S(1)}, f32[4,8,3072]{2,1,0:T(8,128)S(1)}, f32[4,3072]{1,0:T(4,128)S(1)}, /*index=...) while((s32[]{:T(128)}, f32[8,3072]{1,0:T(8,128)S(1)}, ...), condition=%wide.region_9.10_spmd.clone, body=%wide.region_5.9_spmd.clone.sunk | while | flops 9713667 | bytes 7518397 | solution.py:213
  66.0 9.9 %all-gather.2 = f32[32,3072]{1,0:T(8,128)S(1)} all-gather(f32[8,3072]{1,0:T(8,128)S(1)} %get-tuple-element.596), channel_id=4, replica_groups=mesh['seq_0'=2,'seq_1'=4,'seq_2'=4,'grp'=4] {'seq_2'}, dimensions={0}, use_global_device_ids=true | all-gather | bytes 491520 | tf_op jit(solution)/shard_map/all_gather | solution.py:37
  76.6 10.1 %all-gather = f32[32,3072]{1,0:T(8,128)S(1)} all-gather(f32[8,3072]{1,0:T(8,128)S(1)} %get-tuple-element.962), channel_id=2, replica_groups=mesh['seq_0'=2,'seq_1'=4,'seq_2'=4,'grp'=4] {'seq_2'}, dimensions={0}, use_global_device_ids=true | all-gather | bytes 491520 | tf_op jit(solution)/shard_map/all_gather | solution.py:37
  86.8 19.8 %all_gather.54 = f32[4,8,3072]{2,1,0:T(8,128)S(1)} all-gather(f32[1,8,3072]{2,1,0:T(8,128)S(1)} %get-tuple-element.958), channel_id=1, replica_groups=mesh['seq_0'=2,'seq_1'=4,'seq_2'=4,'grp'=4] {'seq_1'}, dimensions={0}, use_global_device_ids=true | all-gather | bytes 491520 | tf_op jit(solution)/shard_map/all_gather | solution.py:37
  106.6 10.0 %all-gather.1 = f32[32,3072]{1,0:T(8,128)S(1)} all-gather(f32[8,3072]{1,0:T(8,128)S(1)} %reduce_sum.138), channel_id=3, replica_groups=mesh['seq_0'=2,'seq_1'=4,'seq_2'=4,'grp'=4] {'seq_2'}, dimensions={0}, use_global_device_ids=true | all-gather | bytes 491520 | tf_op jit(solution)/shard_map/all_gather | solution.py:37
  116.7 9.6 %all_gather.58 = f32[4,8,3072]{2,1,0:T(8,128)S(1)} all-gather(f32[1,8,3072]{2,1,0:T(8,128)S(1)} %bitcast_add_fusion.5), channel_id=1, replica_groups=mesh['seq_0'=2,'seq_1'=4,'seq_2'=4,'grp'=4] {'seq_1'}, dimensions={0}, use_global_device_ids=true | all-gather | bytes 491520 | tf_op jit(solution)/shard_map/all_gather | solution.py:37
  126.4 4.6 all_gather.59
  135.4 9.6 %all_gather.64 = f32[4,8,3072]{2,1,0:T(8,128)S(1)} all-gather(f32[1,8,3072]{2,1,0:T(8,128)S(1)} %get-tuple-element.922), channel_id=1, replica_groups=mesh['seq_0'=2,'seq_1'=4,'seq_2'=4,'grp'=4] {'seq_1'}, dimensions={0}, use_global_device_ids=true | all-gather | bytes 491520 | tf_op jit(solution)/shard_map/all_gather | solution.py:37
  145.0 10.0 %all_gather.60 = f32[4,8,3072]{2,1,0:T(8,128)S(1)} all-gather(f32[1,8,3072]{2,1,0:T(8,128)S(1)} %get-tuple-element.957), channel_id=1, replica_groups=mesh['seq_0'=2,'seq_1'=4,'seq_2'=4,'grp'=4] {'seq_1'}, dimensions={0}, use_global_device_ids=true | all-gather | bytes 491520 | tf_op jit(solution)/shard_map/all_gather | solution.py:37
  168.8 199.6 %while.65 = (s32[]{:T(128)}, f32[8,3072]{1,0:T(8,128)}, f32[8,3072]{1,0:T(8,128)}, bf16[4,32,3072]{2,1,0:T(8,128)(2,1)}, f32[4,32,3072]{2,1,0:T(8,128)}, /*index...) while((s32[]{:T(128)}, f32[8,3072]{1,0:T(8,128)}, ...), condition=%wide.region_18.19_spmd.clone.clone, body=%wide.region_11.18_spmd.clone.clone.sunk | while | flops 135027200 | bytes 161226256 | solution.py:250
  194.9 5.1 multiply_reduce_fusion.11
  242.8 5.1 multiply_reduce_fusion.11
  290.7 5.1 multiply_reduce_fusion.11
  338.7 5.1 multiply_reduce_fusion.11
  378.3 4.9 collective-permute-start.7
  388.2 6.6 collective-permute-done.7
  398.0 103.1 %while.63 = (s32[]{:T(128)}, bf16[12,256,128]{1,2,0:T(8,128)(2,1)S(1)}, f32[12,1280,128]{1,2,0:T(8,128)}, f32[12,1280,128]{1,2,0:T(8,128)}, bf16[12,1280,128]{1,...) while((s32[]{:T(128)}, ...), condition=%wide.region_4.5_spmd, body=%wide.region_0.4_spmd.sunk | while | flops 510165760 | bytes 11622769 | solution.py:140
  520.7 31.4 %collective-permute-done.15 = bf16[12,256,128]{1,2,0:T(8,128)(2,1)} collective-permute-done((bf16[12,256,128]{1,2,0:T(8,128)(2,1)}, bf16[12,256,128]{1,2,0:T(8,128)(2,1)}, u32[]{:S(2)}, u32[]{:S(2)}) %collective-permute-start.15) | collective-permute-done | bytes 786464 | tf_op jit(solution)/shard_map/ppermute | solution.py:23
  553.4 11.0 %collective-permute-done.14 = bf16[12,256,128]{1,2,0:T(8,128)(2,1)} collective-permute-done((bf16[12,256,128]{1,2,0:T(8,128)(2,1)}, bf16[12,256,128]{1,2,0:T(8,128)(2,1)}, u32[]{:S(2)}, u32[]{:S(2)}) %collective-permute-start.14) | collective-permute-done | bytes 786464 | tf_op jit(solution)/shard_map/ppermute | solution.py:23
  568.6 163.3 %all-reduce = (f32[3072]{0:T(1024)}, f32[3072]{0:T(1024)}) all-reduce(f32[3072]{0:T(1024)S(1)} %multiply_reduce_fusion.6, f32[3072]{0:T(1024)S(1)} %multiply_reduce_fusion.5), channel_id=1, replica_groups=mesh['seq_0'=2,'seq_1'=4,'seq_2'=4,'grp'=4] {'seq_0','seq_1','seq_2','grp'}, use_global_device_ids=true, to_apply=%region_21.22 | all-reduce | flops 6144 | bytes 49152 | tf_op jit(solution)/shard_map/psum | solution.py:257
  735.5 4.9 add_convert_fusion
  742.8 30.7 %all-reduce.3.cloned.1.call-done = f32[8,3072]{1,0:T(8,128)} async-done(((f32[8,3072]{1,0:T(8,128)}), f32[8,3072]{1,0:T(8,128)}) %all-reduce.3.cloned.1.call-update) | async-done | bytes 98320 | tf_op jit(solution)/shard_map/psum | solution.py:257
  (527 shorter events, 390.5 us)
Async XLA Ops:
  7.2 26.1 %copy-start.28 = (bf16[1,8,128]{2,1,0:T(8,128)(2,1)S(1)}, bf16[1,8,128]{2,1,0:T(8,128)(2,1)}, u32[]{:S(2)}) copy-start(bf16[1,8,128]{2,1,0:T(8,128)(2,1)} %param.24) | copy-start | bytes 6148
  7.2 27.8 %copy-start.13 = (bf16[1,128,3072]{2,1,0:T(8,128)(2,1)S(1)}, bf16[1,128,3072]{2,1,0:T(8,128)(2,1)}, u32[]{:S(2)}) copy-start(bf16[1,128,3072]{2,1,0:T(8,128)(2,1)} %param.26) | copy-start | bytes 2359300
  7.2 766.2 %all-reduce.3.cloned.1.call-start = ((), (), s32[]{:S(2)}) async-start(), calls=%async_computation | async-start | bytes 196608 | tf_op jit(solution)/shard_map/psum | solution.py:257
  9.7 361.6 %collective-permute-start = (bf16[256,1536]{0,1:T(8,128)(2,1)}, bf16[256,1536]{0,1:T(8,128)(2,1)}, u32[]{:S(2)}, u32[]{:S(2)}) collective-permute-start(bf16[256,1536]{0,1:T(8,128)(2,1)} %bitcast.16), channel_id=1, source_target_pairs={{0,16},{4,20},{8,24},{12,28},{16,32},{20,36},{24,40},{28,44},{32,4... | collective-permute-start | bytes 2359304 | tf_op jit(solution)/shard_map/ppermute | solution.py:23
  14.6 363.8 %collective-permute-start.1 = (bf16[256,1536]{0,1:T(8,128)(2,1)}, bf16[256,1536]{0,1:T(8,128)(2,1)}, u32[]{:S(2)}, u32[]{:S(2)}) collective-permute-start(bf16[256,1536]{0,1:T(8,128)(2,1)} %bitcast.16), channel_id=1, source_target_pairs={{0,12},{4,16},{8,20},{12,24},{16,28},{20,32},{24,36},{28,40},{32,4... | collective-permute-start | bytes 2359304 | tf_op jit(solution)/shard_map/ppermute | solution.py:23
  19.8 364.6 %collective-permute-start.2 = (bf16[256,1536]{0,1:T(8,128)(2,1)}, bf16[256,1536]{0,1:T(8,128)(2,1)}, u32[]{:S(2)}, u32[]{:S(2)}) collective-permute-start(bf16[256,1536]{0,1:T(8,128)(2,1)} %bitcast.16), channel_id=1, source_target_pairs={{0,8},{4,12},{8,16},{12,20},{16,24},{20,28},{24,32},{28,36},{32,40... | collective-permute-start | bytes 2359304 | tf_op jit(solution)/shard_map/ppermute | solution.py:23
  23.3 362.3 %collective-permute-start.3 = (bf16[256,1536]{0,1:T(8,128)(2,1)}, bf16[256,1536]{0,1:T(8,128)(2,1)}, u32[]{:S(2)}, u32[]{:S(2)}) collective-permute-start(bf16[256,1536]{0,1:T(8,128)(2,1)} %bitcast.16), channel_id=1, source_target_pairs={{0,4},{4,8},{8,12},{12,16},{16,20},{20,24},{24,28},{28,32},{32,36}... | collective-permute-start | bytes 2359304 | tf_op jit(solution)/shard_map/ppermute | solution.py:23
  28.1 346.5 %collective-permute-start.4 = (bf16[256,1536]{0,1:T(8,128)(2,1)}, bf16[256,1536]{0,1:T(8,128)(2,1)}, u32[]{:S(2)}, u32[]{:S(2)}) collective-permute-start(bf16[256,1536]{0,1:T(8,128)(2,1)} %bitcast.27), channel_id=1, source_target_pairs={{0,16},{4,20},{8,24},{12,28},{16,32},{20,36},{24,40},{28,44},{32,4... | collective-permute-start | bytes 2359304 | tf_op jit(solution)/shard_map/ppermute | solution.py:23
  371.2 16.8 %collective-permute-start.5 = (bf16[256,1536]{0,1:T(8,128)(2,1)}, bf16[256,1536]{0,1:T(8,128)(2,1)S(1)}, u32[]{:S(2)}, u32[]{:S(2)}) collective-permute-start(bf16[256,1536]{0,1:T(8,128)(2,1)} %bitcast.27), channel_id=1, source_target_pairs={{0,12},{4,16},{8,20},{12,24},{16,28},{20,32},{24,36},{28,40},{32,4... | collective-permute-start | bytes 2359304 | tf_op jit(solution)/shard_map/ppermute | solution.py:23
  374.7 13.4 %collective-permute-start.6 = (bf16[256,1536]{0,1:T(8,128)(2,1)}, bf16[256,1536]{0,1:T(8,128)(2,1)S(1)}, u32[]{:S(2)}, u32[]{:S(2)}) collective-permute-start(bf16[256,1536]{0,1:T(8,128)(2,1)} %bitcast.27), channel_id=1, source_target_pairs={{0,8},{4,12},{8,16},{12,20},{16,24},{20,28},{24,32},{28,36},{32,40... | collective-permute-start | bytes 2359304 | tf_op jit(solution)/shard_map/ppermute | solution.py:23
  378.3 16.5 %collective-permute-start.7 = (bf16[256,1536]{0,1:T(8,128)(2,1)}, bf16[256,1536]{0,1:T(8,128)(2,1)S(1)}, u32[]{:S(2)}, u32[]{:S(2)}) collective-permute-start(bf16[256,1536]{0,1:T(8,128)(2,1)} %bitcast.27), channel_id=1, source_target_pairs={{0,4},{4,8},{8,12},{12,16},{16,20},{20,24},{24,28},{28,32},{32,36}... | collective-permute-start | bytes 2359304 | tf_op jit(solution)/shard_map/ppermute | solution.py:23
  507.5 44.6 %collective-permute-start.15 = (bf16[12,256,128]{1,2,0:T(8,128)(2,1)}, bf16[12,256,128]{1,2,0:T(8,128)(2,1)}, u32[]{:S(2)}, u32[]{:S(2)}) collective-permute-start(bf16[12,256,128]{1,2,0:T(8,128)(2,1)} %get-tuple-element.949), channel_id=1, source_target_pairs={{16,0},{20,4},{24,8},{28,12},{32,16},{36,20},{40,24},{44,28},{48,3... | collective-permute-start | bytes 2359304 | tf_op jit(solution)/shard_map/ppermute | solution.py:23
  508.9 55.5 %collective-permute-start.14 = (bf16[12,256,128]{1,2,0:T(8,128)(2,1)}, bf16[12,256,128]{1,2,0:T(8,128)(2,1)}, u32[]{:S(2)}, u32[]{:S(2)}) collective-permute-start(bf16[12,256,128]{1,2,0:T(8,128)(2,1)} %get-tuple-element.950), channel_id=1, source_target_pairs={{12,0},{16,4},{20,8},{24,12},{28,16},{32,20},{36,24},{40,28},{44,3... | collective-permute-start | bytes 2359304 | tf_op jit(solution)/shard_map/ppermute | solution.py:23
  510.2 55.4 %collective-permute-start.13 = (bf16[12,256,128]{1,2,0:T(8,128)(2,1)}, bf16[12,256,128]{1,2,0:T(8,128)(2,1)}, u32[]{:S(2)}, u32[]{:S(2)}) collective-permute-start(bf16[12,256,128]{1,2,0:T(8,128)(2,1)} %get-tuple-element.951), channel_id=1, source_target_pairs={{8,0},{12,4},{16,8},{20,12},{24,16},{28,20},{32,24},{36,28},{40,32... | collective-permute-start | bytes 2359304 | tf_op jit(solution)/shard_map/ppermute | solution.py:23
  512.7 222.8 %collective-permute-start.12 = (bf16[12,256,128]{1,2,0:T(8,128)(2,1)}, bf16[12,256,128]{1,2,0:T(8,128)(2,1)}, u32[]{:S(2)}, u32[]{:S(2)}) collective-permute-start(bf16[12,256,128]{1,2,0:T(8,128)(2,1)} %get-tuple-element.948), channel_id=1, source_target_pairs={{4,0},{8,4},{12,8},{16,12},{20,16},{24,20},{28,24},{32,28},{36,32}... | collective-permute-start | bytes 2359304 | tf_op jit(solution)/shard_map/ppermute | solution.py:23
  517.7 49.3 %copy-start.12 = (bf16[1,128,3072]{2,1,0:T(8,128)(2,1)S(1)}, bf16[1,128,3072]{2,1,0:T(8,128)(2,1)}, u32[]{:S(2)}) copy-start(bf16[1,128,3072]{2,1,0:T(8,128)(2,1)} %param.22) | copy-start | bytes 2359300
  517.7 49.3 %copy-start.14 = (bf16[1,128,3072]{2,1,0:T(8,128)(2,1)S(1)}, bf16[1,128,3072]{2,1,0:T(8,128)(2,1)}, u32[]{:S(2)}) copy-start(bf16[1,128,3072]{2,1,0:T(8,128)(2,1)} %param.26) | copy-start | bytes 2359300
  517.7 49.5 %copy-start.24 = (bf16[4,32,8]{2,1,0:T(8,128)(2,1)S(1)}, bf16[4,32,8]{2,1,0:T(8,128)(2,1)}, u32[]{:S(2)}) copy-start(bf16[4,32,8]{2,1,0:T(8,128)(2,1)} %get-tuple-element.599) | copy-start | bytes 6148
  517.7 50.2 %copy-start.25 = (bf16[4,32,8]{2,1,0:T(8,128)(2,1)S(1)}, bf16[4,32,8]{2,1,0:T(8,128)(2,1)}, u32[]{:S(2)}) copy-start(bf16[4,32,8]{2,1,0:T(8,128)(2,1)} %get-tuple-element.600) | copy-start | bytes 6148
  517.7 214.2 %copy-start.16 = (bf16[1,128,3072]{2,1,0:T(8,128)(2,1)S(1)}, bf16[1,128,3072]{2,1,0:T(8,128)(2,1)}, u32[]{:S(2)}) copy-start(bf16[1,128,3072]{2,1,0:T(8,128)(2,1)} %param.23) | copy-start | bytes 2359300
  519.3 216.2 %collective-permute-start.11 = (bf16[12,256,128]{1,2,0:T(8,128)(2,1)}, bf16[12,256,128]{1,2,0:T(8,128)(2,1)}, u32[]{:S(2)}, u32[]{:S(2)}) collective-permute-start(bf16[12,256,128]{1,2,0:T(8,128)(2,1)} %get-tuple-element.953), channel_id=1, source_target_pairs={{16,0},{20,4},{24,8},{28,12},{32,16},{36,20},{40,24},{44,28},{48,3... | collective-permute-start | bytes 2359304 | tf_op jit(solution)/shard_map/ppermute | solution.py:23
  552.1 183.4 %collective-permute-start.10 = (bf16[12,256,128]{1,2,0:T(8,128)(2,1)}, bf16[12,256,128]{1,2,0:T(8,128)(2,1)}, u32[]{:S(2)}, u32[]{:S(2)}) collective-permute-start(bf16[12,256,128]{1,2,0:T(8,128)(2,1)} %get-tuple-element.954), channel_id=1, source_target_pairs={{12,0},{16,4},{20,8},{24,12},{28,16},{32,20},{36,24},{40,28},{44,3... | collective-permute-start | bytes 2359304 | tf_op jit(solution)/shard_map/ppermute | solution.py:23
  564.4 171.1 %collective-permute-start.9 = (bf16[12,256,128]{1,2,0:T(8,128)(2,1)}, bf16[12,256,128]{1,2,0:T(8,128)(2,1)}, u32[]{:S(2)}, u32[]{:S(2)}) collective-permute-start(bf16[12,256,128]{1,2,0:T(8,128)(2,1)} %get-tuple-element.955), channel_id=1, source_target_pairs={{8,0},{12,4},{16,8},{20,12},{24,16},{28,20},{32,24},{36,28},{40,32... | collective-permute-start | bytes 2359304 | tf_op jit(solution)/shard_map/ppermute | solution.py:23
  565.7 169.8 %collective-permute-start.8 = (bf16[12,256,128]{1,2,0:T(8,128)(2,1)S(1)}, bf16[12,256,128]{1,2,0:T(8,128)(2,1)}, u32[]{:S(2)}, u32[]{:S(2)}) collective-permute-start(bf16[12,256,128]{1,2,0:T(8,128)(2,1)S(1)} %get-tuple-element.952), channel_id=1, source_target_pairs={{4,0},{8,4},{12,8},{16,12},{20,16},{24,20},{28,24},{32,28},{36,32}... | collective-permute-start | bytes 2359304 | tf_op jit(solution)/shard_map/ppermute | solution.py:23
  (53 other events, 217.7 us)
Sparse Core Ops, SparseCore 0:
  512.4 261.0 all-reduce.2
where the time goes:
time: 796 us; the launch traced here: 782 us
  blocking collectives  260 us (33%)
  local copies, waits for them, and re-layouts  144 us (18%)
  other arithmetic  131 us (16%)
  matrix products  104 us (13%)
  waiting for transfers between devices  79.7 us (10%)
  starting transfers between devices  38.6 us (5%)
  between operations  14.8 us (2%)
  loops' own time  9.63 us (1%)
    psum x1, blocking collectives, mixer_part(): lax.psum((rate_grad * decay_rate, jnp.sum(grad_raw, axis=0), jnp.sum(cot_...  163 us
    all_gather x11, blocking collectives, carried_in(): pieces = jax.tree.map(lambda part: lax.all_gather(part, axis), subtotal)  96.6 us
    while x132, local copies, waits for them, and re-layouts  73.4 us
    ppermute x16, waiting for transfers between devices, shifted(): return lax.ppermute(block, axis, route)  49 us
    ppermute x16, starting transfers between devices, shifted(): return lax.ppermute(block, axis, route)  38.6 us
    psum x1, waiting for transfers between devices, mixer_part(): lax.psum((rate_grad * decay_rate, jnp.sum(grad_raw, axis=0), jnp.sum(cot_...  30.7 us
    unnamed x58, local copies, waits for them, and re-layouts  24.4 us
    reduce_sum x4, other arithmetic, block_back(): grad_in = jnp.sum(adjoint * (step_blk * input_blk)[:, None, :], axis=2)  20.3 us
  transfers between devices with their start and end apart: 17, of which 4 were waited for; matrix products, arithmetic and copies ran while one was open for 33% of the time, Pallas kernels for 0%

commit v1 on v0

v1 whole, which is shorter than its diff:
```python
import functools

import jax
import jax.numpy as jnp
from jax import lax
from jax.experimental import pallas as pl
from jax.experimental.pallas import tpu as pltpu
from jax.sharding import PartitionSpec as P

MESH = pl.DeviceIdType.MESH
F32 = jnp.float32
BF16 = jnp.bfloat16

NSEQ = 32
NGRP = 4
ROW = 4
NROW = NSEQ // ROW
BLK = 256
OWN = ROW * BLK
HPD = 3
HD = 128
TOK = 128
NCH = 8
LEN = TOK // NCH
PITCH = 24
NST = 8
TILES = 24
INNER = TILES * 128
LOG2E = 1.4426950408889634
LN2 = 0.6931471805599453
NEG = -1e30
SCALE = HD**-0.5

NT = (((1,), (1,)), ((), ()))
NN = (((1,), (0,)), ((), ()))
TN = (((0,), (0,)), ((), ()))


def dot(a, b, dims):
    return lax.dot_general(a, b, dims, preferred_element_type=F32)


def kernel(
    q_hbm, k_hbm, v_hbm, do_hbm, x_ref, raw_ref, bin_ref, cout_ref, cot_ref, dl_ref, bias_ref, skip_ref,
    dq_hbm, dk_hbm, dv_hbm, gx_ref, gr_ref, gin_ref, gout_ref, gdec_ref, gbias_ref, gskip_ref,
    qs, dos, ks, vs, acc, qout, retout, retin, fin,
    dts, xs, cts, sgs, avs, a2s, btab, ctab, natt, tscr, pds, pes, sds, sbs, tot, gath, cbuf, cin,
    ahs, gxt, grt, gbacc, gcacc, gred, par, pgat, psm, p4, pfin, pout,
    in_send, in_recv, in_loc, fw_send, fw_recv, rt_send, rt_recv, q_send, q_recv, o_send, o_recv, o_loc,
    a_send, a_recv, b_send, b_recv, c_send, c_recv, d_send, d_recv, e_send, e_recv,
):
    s = lax.axis_index("seq")
    g = lax.axis_index("grp")
    col = lax.rem(s, ROW)
    base = s - col
    row = s // ROW
    first = row == 0
    last = row == NROW - 1

    barrier = pltpu.get_barrier_semaphore()

    @pl.loop(0, NSEQ)
    def _(i):
        @pl.when(i != s)
        def _():
            pl.semaphore_signal(barrier, inc=1, device_id={"seq": i}, device_id_type=MESH)

    @pl.loop(0, NGRP)
    def _(i):
        @pl.when(i != g)
        def _():
            pl.semaphore_signal(barrier, inc=1, device_id={"grp": i}, device_id_type=MESH)

    pl.semaphore_wait(barrier, NSEQ + NGRP - 2)

    srcs = (k_hbm, v_hbm, q_hbm, do_hbm)
    dsts = (ks, vs, qs, dos)
    lead = (OWN, OWN, 0, 0)

    def in_copy(t, h, off):
        peer = lax.rem(col + off, ROW)
        lanes = pl.ds(pl.multiple_of((peer * HPD + h) * HD, HD), HD)
        rows = pl.ds(pl.multiple_of(lead[t] + col * BLK, BLK), BLK)
        return pltpu.make_async_remote_copy(
            src_ref=srcs[t].at[0, :, lanes],
            dst_ref=dsts[t].at[h, rows, :],
            send_sem=in_send.at[t, h, off - 1],
            recv_sem=in_recv.at[t, h, off - 1],
            device_id={"seq": base + peer},
            device_id_type=MESH,
        )

    def in_wait(t, h, off):
        peer = lax.rem(col + ROW - off, ROW)
        lanes = pl.ds(pl.multiple_of((col * HPD + h) * HD, HD), HD)
        rows = pl.ds(pl.multiple_of(lead[t] + peer * BLK, BLK), BLK)
        pltpu.make_async_remote_copy(
            src_ref=srcs[t].at[0, :, lanes],
            dst_ref=dsts[t].at[h, rows, :],
            send_sem=in_send.at[t, h, off - 1],
            recv_sem=in_recv.at[t, h, off - 1],
            device_id={"seq": base + peer},
            device_id_type=MESH,
        ).wait_recv()

    def in_local(t, h):
        lanes = pl.ds(pl.multiple_of((col * HPD + h) * HD, HD), HD)
        rows = pl.ds(pl.multiple_of(lead[t] + col * BLK, BLK), BLK)
        return pltpu.make_async_copy(
            srcs[t].at[0, :, lanes], dsts[t].at[h, rows, :], in_loc.at[t, h]
        )

    def send_in(h):
        for t in range(4):
            for off in range(1, ROW):
                in_copy(t, h, off).start()
            in_local(t, h).start()

    def fw_copy(t, h):
        return pltpu.make_async_remote_copy(
            src_ref=dsts[t].at[h, pl.ds(OWN, OWN), :],
            dst_ref=dsts[t].at[h, pl.ds(0, OWN), :],
            send_sem=fw_send.at[t, h],
            recv_sem=fw_recv.at[t, h],
            device_id={"seq": lax.rem(s + ROW, NSEQ)},
            device_id_type=MESH,
        )

    def forward_kv(h):
        for t in range(2):
            for off in range(1, ROW):
                in_wait(t, h, off)
            in_local(t, h).wait()

            @pl.when(jnp.logical_not(last))
            def _():
                fw_copy(t, h).start()

    def rt_copy(t, h):
        return pltpu.make_async_remote_copy(
            src_ref=retout.at[h, t],
            dst_ref=retin.at[h, t],
            send_sem=rt_send.at[t, h],
            recv_sem=rt_recv.at[t, h],
            device_id={"seq": lax.rem(s + NSEQ - ROW, NSEQ)},
            device_id_type=MESH,
        )

    outs = (dk_hbm, dv_hbm)

    def out_copy(src, dst, h, off, send, recv):
        peer = lax.rem(col + off, ROW)
        lanes = pl.ds(pl.multiple_of((col * HPD + h) * HD, HD), HD)
        rows = pl.ds(pl.multiple_of(peer * BLK, BLK), BLK)
        return pltpu.make_async_remote_copy(
            src_ref=src.at[rows, :],
            dst_ref=dst.at[0, :, lanes],
            send_sem=send,
            recv_sem=recv,
            device_id={"seq": base + peer},
            device_id_type=MESH,
        )

    def out_wait(src, dst, h, off, send, recv):
        peer = lax.rem(col + ROW - off, ROW)
        lanes = pl.ds(pl.multiple_of((peer * HPD + h) * HD, HD), HD)
        pltpu.make_async_remote_copy(
            src_ref=src.at[pl.ds(0, BLK), :],
            dst_ref=dst.at[0, :, lanes],
            send_sem=send,
            recv_sem=recv,
            device_id={"seq": base + peer},
            device_id_type=MESH,
        ).wait_recv()

    def out_local(src, dst, h, sem):
        lanes = pl.ds(pl.multiple_of((col * HPD + h) * HD, HD), HD)
        rows = pl.ds(pl.multiple_of(col * BLK, BLK), BLK)
        return pltpu.make_async_copy(src.at[rows, :], dst.at[0, :, lanes], sem)

    def attention(h):
        for t in range(2, 4):
            for off in range(1, ROW):
                in_wait(t, h, off)
            in_local(t, h).wait()

        @pl.when(jnp.logical_not(first))
        def _():
            for t in range(2):
                fw_copy(t, h).wait_recv()

        @pl.when(first)
        def _():
            zeros = jnp.zeros((OWN, HD), BF16)
            ks[h, pl.ds(0, OWN), :] = zeros
            vs[h, pl.ds(0, OWN), :] = zeros

        acc[h] = jnp.zeros(acc.shape[1:], F32)
        key_pos = lax.broadcasted_iota(jnp.int32, (BLK, BLK), 0)
        qry_pos = lax.broadcasted_iota(jnp.int32, (BLK, BLK), 1)
        causal = key_pos <= qry_pos

        @pl.loop(0, ROW)
        def _(i):
            at = pl.multiple_of(i * BLK, BLK)
            qrows = pl.ds(at, BLK)
            krows = pl.ds(at, OWN + BLK)
            qb = qs[h, qrows, :]
            dob = dos[h, qrows, :]
            kb = ks[h, krows, :]
            vb = vs[h, krows, :]
            st = dot(kb, qb, NT)
            dpt = dot(vb, dob, NT)

            def bias(kt):
                return jnp.where(jnp.logical_and(first, i + kt < ROW), NEG, 0.0).astype(F32)

            parts = [jnp.where(causal, st[OWN:], st[:BLK] + bias(0))]
            for kt in range(1, ROW):
                parts.append(st[kt * BLK : (kt + 1) * BLK] + bias(kt))
            scores = jnp.concatenate(parts, 0)
            dp = jnp.concatenate([jnp.where(causal, dpt[OWN:], dpt[:BLK]), dpt[BLK:OWN]], 0)
            top = jnp.max(scores, axis=0, keepdims=True)
            raw = jnp.exp2((scores - top) * (SCALE * LOG2E))
            prob = raw * (1.0 / jnp.sum(raw, axis=0, keepdims=True))
            pb = prob.astype(BF16)
            delta = jnp.sum(pb.astype(F32) * dp, axis=0, keepdims=True)
            ds = prob * (dp - delta)
            zero = jnp.zeros((BLK, BLK), F32)
            pfull = jnp.concatenate(
                [jnp.where(causal, zero, prob[:BLK]).astype(BF16), pb[BLK:], jnp.where(causal, prob[:BLK], zero).astype(BF16)], 0
            )
            dsb = ds.astype(BF16)
            dfull = jnp.concatenate(
                [jnp.where(causal, zero, ds[:BLK]).astype(BF16), dsb[BLK:], jnp.where(causal, ds[:BLK], zero).astype(BF16)], 0
            )
            acc[h, 1, krows, :] += dot(pfull, dob, NN)
            acc[h, 0, krows, :] += dot(dfull, qb, NN)
            dq = dot(kb, dfull, TN)
            qout[h, qrows, :] = (dq.T * SCALE).astype(BF16)

        for off in range(1, ROW):
            out_copy(qout.at[h], dq_hbm, h, off, q_send.at[h, off - 1], q_recv.at[h, off - 1]).start()
        out_local(qout.at[h], dq_hbm, h, o_loc.at[2, h]).start()

        @pl.when(jnp.logical_not(first))
        def _():
            retout[h, 0] = (acc[h, 0, pl.ds(0, OWN), :] * SCALE).astype(BF16)
            rt_copy(0, h).start()
            retout[h, 1] = acc[h, 1, pl.ds(0, OWN), :].astype(BF16)
            rt_copy(1, h).start()

    def finish_head(h):
        for t in range(2):
            scale = SCALE if t == 0 else 1.0

            @pl.when(last)
            def _():
                fin[h, t] = (acc[h, t, pl.ds(OWN, OWN), :] * scale).astype(BF16)

            @pl.when(jnp.logical_not(last))
            def _():
                rt_copy(t, h).wait_recv()
                own = acc[h, t, pl.ds(OWN, OWN), :] * scale
                fin[h, t] = (own + retin[h, t].astype(F32)).astype(BF16)

            for off in range(1, ROW):
                out_copy(fin.at[h, t], outs[t], h, off, o_send.at[t, h, off - 1], o_recv.at[t, h, off - 1]).start()
            out_local(fin.at[h, t], outs[t], h, o_loc.at[t, h]).start()

    def drain():
        @pl.loop(0, HPD)
        def _(h):
            for t in range(4):
                for off in range(1, ROW):
                    in_copy(t, h, off).wait_send()
            for off in range(1, ROW):
                out_copy(qout.at[h], dq_hbm, h, off, q_send.at[h, off - 1], q_recv.at[h, off - 1]).wait_send()
                out_wait(qout.at[h], dq_hbm, h, off, q_send.at[h, off - 1], q_recv.at[h, off - 1])
            out_local(qout.at[h], dq_hbm, h, o_loc.at[2, h]).wait()
            for t in range(2):

                @pl.when(jnp.logical_not(last))
                def _():
                    fw_copy(t, h).wait_send()

                @pl.when(jnp.logical_not(first))
                def _():
                    rt_copy(t, h).wait_send()

                for off in range(1, ROW):
                    sems = (o_send.at[t, h, off - 1], o_recv.at[t, h, off - 1])
                    out_copy(fin.at[h, t], outs[t], h, off, *sems).wait_send()
                    out_wait(fin.at[h, t], outs[t], h, off, *sems)
                out_local(fin.at[h, t], outs[t], h, o_loc.at[t, h]).wait()

    def mixer_tables():
        bin32 = bin_ref[0].astype(F32)
        cout32 = cout_ref[0].astype(F32)
        for tab, rows32 in ((btab, bin32), (ctab, cout32)):
            for n in range(NST):
                wide = jnp.broadcast_to(rows32[n : n + 1, :], (TOK, TOK)).T
                for k in range(NCH):
                    natt[pl.ds(k * PITCH, LEN), :] = wide[k * LEN : (k + 1) * LEN]
                for j in range(LEN):
                    tab[n, j] = natt[pl.ds(j, NCH, stride=PITCH), :]

    def spread(block, n):
        return jnp.broadcast_to(block[n : n + 1, :], (NCH, 128))

    def mixer_local(c):
        lanes = pl.ds(pl.multiple_of(c * 128, 128), 128)
        x = x_ref[0, :, lanes].astype(F32)
        z = raw_ref[0, :, lanes].astype(F32) + bias_ref[:, lanes]
        ct = cot_ref[0, :, lanes].astype(F32)
        small = jnp.exp(-jnp.abs(z))
        dt = jnp.maximum(z, 0.0) + jnp.log1p(small)
        sg = jnp.where(z >= 0.0, 1.0, small) / (1.0 + small)
        par[c, 9:10, :] = jnp.sum(ct * x, axis=0, keepdims=True)
        for k in range(NCH):
            rows = pl.ds(k * PITCH, LEN)
            part = slice(k * LEN, (k + 1) * LEN)
            dts[c, rows, :] = dt[part]
            xs[c, rows, :] = x[part]
            cts[c, rows, :] = ct[part]
            sgs[c, rows, :] = sg[part]
        a2 = -jnp.exp(dl_ref[:, lanes]) * LOG2E
        a2s[c] = a2
        rate = [spread(a2, n) for n in range(NST)]
        state = [jnp.zeros((NCH, 128), F32) for _ in range(NST)]
        decay = [jnp.ones((NCH, 128), F32) for _ in range(NST)]
        back = [jnp.zeros((NCH, 128), F32) for _ in range(NST)]
        for j in range(LEN):
            rows = pl.ds(j, NCH, stride=PITCH)
            dtj = dts[c, rows, :]
            uj = dtj * xs[c, rows, :]
            cj = cts[c, rows, :]
            for n in range(NST):
                a = jnp.exp2(dtj * rate[n])
                avs[c, j, n] = a
                state[n] = a * state[n] + uj * btab[n, j]
                decay[n] = a * decay[n]
                back[n] = back[n] + decay[n] * (cj * ctab[n, j])
        for n in range(NST):
            rows = pl.ds(n * NCH, NCH)
            tscr[0, rows, :] = state[n]
            tscr[1, rows, :] = decay[n]
            tscr[2, rows, :] = back[n]
        ek = [tscr[0, pl.ds(k, NST, stride=NCH), :] for k in range(NCH)]
        dk = [tscr[1, pl.ds(k, NST, stride=NCH), :] for k in range(NCH)]
        bk = [tscr[2, pl.ds(k, NST, stride=NCH), :] for k in range(NCH)]
        pd = jnp.ones((NST, 128), F32)
        pe = jnp.zeros((NST, 128), F32)
        for k in range(NCH):
            pds[c, k] = pd
            pes[c, k] = pe
            pe = dk[k] * pe + ek[k]
            pd = dk[k] * pd
        sd = jnp.ones((NST, 128), F32)
        sb = jnp.zeros((NST, 128), F32)
        for k in reversed(range(NCH)):
            sds[c, k] = sd
            sbs[c, k] = sb
            sb = dk[k] * sb + bk[k]
            sd = dk[k] * sd
        tot[c, 0:8, :] = pe
        tot[c, 8:16, :] = pd
        tot[c, 16:24, :] = sb

    def scatter(src, dst, send, recv):
        @pl.loop(0, TILES)
        def _(j):
            @pl.when(j != s)
            def _():
                pltpu.make_async_remote_copy(
                    src_ref=src.at[j], dst_ref=dst.at[s], send_sem=send, recv_sem=recv,
                    device_id={"seq": j}, device_id_type=MESH,
                ).start()

        @pl.when(s < TILES)
        def _():
            dst[s] = src[s]

    def scatter_wait_recv(dst, sem):
        head = dst.at[pl.ds(0, NSEQ - 1)]
        pltpu.make_async_copy(head, head, sem).wait()

    def tiles_wait(ref, sem):
        @pl.when(s < TILES)
        def _():
            part = ref.at[pl.ds(0, TILES - 1)]
            pltpu.make_async_copy(part, part, sem).wait()

        @pl.when(s >= TILES)
        def _():
            part = ref.at[pl.ds(0, TILES)]
            pltpu.make_async_copy(part, part, sem).wait()

    def spread_out(src_of, dst, send, recv):
        @pl.loop(0, NSEQ)
        def _(i):
            @pl.when(i != s)
            def _():
                pltpu.make_async_remote_copy(
                    src_ref=src_of(i), dst_ref=dst.at[s], send_sem=send, recv_sem=recv,
                    device_id={"seq": i}, device_id_type=MESH,
                ).start()

    def mixer_prefix():
        @pl.when(s < TILES)
        def _():
            scatter_wait_recv(gath, a_recv)
            carry = jnp.zeros((NST, 128), F32)
            for i in range(NSEQ):
                cbuf[i, 0:8, :] = carry
                carry = gath[i, 8:16, :] * carry + gath[i, 0:8, :]
            carry = jnp.zeros((NST, 128), F32)
            for i in reversed(range(NSEQ)):
                cbuf[i, 8:16, :] = carry
                carry = gath[i, 8:16, :] * carry + gath[i, 16:24, :]
            spread_out(lambda i: cbuf.at[i], cin, b_send, b_recv)
            cin[s] = cbuf[s]

    def mixer_back(c):
        lanes = pl.ds(pl.multiple_of(c * 128, 128), 128)
        hin = cin[c, 0:8, :]
        gin = cin[c, 8:16, :]
        for k in range(NCH):
            rows = pl.ds(k * NST, NST)
            tscr[0, rows, :] = pds[c, k] * hin + pes[c, k]
            tscr[1, rows, :] = sds[c, k] * gin + sbs[c, k]
        state = [tscr[0, pl.ds(n, NCH, stride=NST), :] for n in range(NST)]
        a2 = a2s[c]
        for j in range(LEN):
            rows = pl.ds(j, NCH, stride=PITCH)
            uj = dts[c, rows, :] * xs[c, rows, :]
            cj = cts[c, rows, :]
            for n in range(NST):
                ah = avs[c, j, n] * state[n]
                ahs[j, n] = ah
                state[n] = ah + uj * btab[n, j]
                gcacc[n, pl.ds(j * NCH, NCH), :] += cj * state[n]
        adj = [tscr[1, pl.ds(n, NCH, stride=NST), :] for n in range(NST)]
        ga = [jnp.zeros((NCH, 128), F32) for _ in range(NST)]
        rate = [spread(a2, n) for n in range(NST)]
        skip = jnp.broadcast_to(skip_ref[:, lanes], (NCH, 128))
        gb = jnp.zeros((NCH, 128), F32)
        for j in reversed(range(LEN)):
            rows = pl.ds(j, NCH, stride=PITCH)
            dtj = dts[c, rows, :]
            xj = xs[c, rows, :]
            uj = dtj * xj
            cj = cts[c, rows, :]
            proj = None
            gdt = None
            for n in range(NST):
                gn = adj[n] + ctab[n, j] * cj
                gbacc[n, pl.ds(j * NCH, NCH), :] += gn * uj
                w = gn * ahs[j, n]
                ga[n] = ga[n] + w * dtj
                p1 = gn * btab[n, j]
                p2 = w * rate[n]
                proj = p1 if proj is None else proj + p1
                gdt = p2 if gdt is None else gdt + p2
                adj[n] = avs[c, j, n] * gn
            gxt[rows, :] = skip * cj + dtj * proj
            graw = (xj * proj + gdt * LN2) * sgs[c, rows, :]
            grt[rows, :] = graw
            gb = gb + graw
        for n in range(NST):
            tscr[2, pl.ds(n * NCH, NCH), :] = ga[n]
        gsum = tscr[2, pl.ds(0, NST, stride=NCH), :]
        for k in range(1, NCH):
            gsum = gsum + tscr[2, pl.ds(k, NST, stride=NCH), :]
        par[c, 0:8, :] = gsum * (a2 * LN2)
        par[c, 8:9, :] = jnp.sum(gb, axis=0, keepdims=True)
        for k in range(NCH):
            rows = pl.ds(k * PITCH, LEN)
            gx_ref[0, pl.ds(k * LEN, LEN), lanes] = gxt[rows, :].astype(BF16)
            gr_ref[0, pl.ds(k * LEN, LEN), lanes] = grt[rows, :].astype(BF16)

    def mixer_state_grads():
        ones = jnp.ones((8, 128), F32)
        for accum, ref in ((gbacc, gin_ref), (gcacc, gout_ref)):
            for n in range(NST):
                rows = [accum[n, pl.ds(k, LEN, stride=NCH), :] for k in range(NCH)]
                full = jnp.concatenate(rows, 0)
                line = lax.dot_general(
                    ones, full, NT, preferred_element_type=F32, precision=lax.Precision.HIGHEST
                )
                gred[n : n + 1, :] = line[0:1, :]
            ref[0] = gred[...].astype(BF16)

    def params_rows():
        @pl.when(s < TILES)
        def _():
            scatter_wait_recv(pgat, c_recv)
            total = pgat[0]
            for i in range(1, NSEQ):
                total = total + pgat[i]
            psm[...] = total
            p4[g] = total

            @pl.loop(0, NGRP)
            def _(i):
                @pl.when(i != g)
                def _():
                    pltpu.make_async_remote_copy(
                        src_ref=psm, dst_ref=p4.at[g], send_sem=d_send, recv_sem=d_recv,
                        device_id={"grp": i}, device_id_type=MESH,
                    ).start()

    def params_groups():
        @pl.when(s < TILES)
        def _():
            head = p4.at[pl.ds(0, NGRP - 1)]
            pltpu.make_async_copy(head, head, d_recv).wait()
            final = (p4[0] + p4[1]) + (p4[2] + p4[3])
            pfin[...] = final
            pout[s] = final
            spread_out(lambda i: pfin, pout, e_send, e_recv)

    def params_store():
        tiles_wait(pout, e_recv)

        @pl.loop(0, TILES)
        def _(c):
            lanes = pl.ds(pl.multiple_of(c * 128, 128), 128)
            gdec_ref[:, lanes] = pout[c, 0:8, :]
            gbias_ref[:, lanes] = pout[c, 8:9, :]
            gskip_ref[:, lanes] = pout[c, 9:10, :]

    def mixer_drain():
        tiles_wait(tot, a_send)
        tiles_wait(par, c_send)

        @pl.when(s < TILES)
        def _():
            part = cbuf.at[pl.ds(0, NSEQ - 1)]
            pltpu.make_async_copy(part, part, b_send).wait()
            part = p4.at[pl.ds(0, NGRP - 1)]
            pltpu.make_async_copy(part, part, d_send).wait()
            part = pgat.at[pl.ds(0, NSEQ - 1)]
            pltpu.make_async_copy(part, part, e_send).wait()

    send_in(0)
    mixer_tables()

    @pl.loop(0, TILES)
    def _(c):
        mixer_local(c)

    scatter(tot, gath, a_send, a_recv)
    send_in(1)
    send_in(2)
    forward_kv(0)
    mixer_prefix()
    gbacc[...] = jnp.zeros(gbacc.shape, F32)
    gcacc[...] = jnp.zeros(gcacc.shape, F32)
    par[:, 10:16, :] = jnp.zeros((TILES, 6, 128), F32)
    forward_kv(1)
    tiles_wait(cin, b_recv)

    @pl.loop(0, TILES)
    def _(c):
        mixer_back(c)

    scatter(par, pgat, c_send, c_recv)
    forward_kv(2)
    mixer_state_grads()
    params_rows()
    attention(0)
    params_groups()
    attention(1)
    finish_head(0)
    params_store()
    attention(2)
    finish_head(1)
    mixer_drain()
    finish_head(2)
    drain()


def per_device(queries, keys, values, cot_attn, x, raw, bin_, cout, cot, decay_log, step_bias, skip_gain):
    vm = pl.BlockSpec(memory_space=pltpu.VMEM)
    hbm = pl.BlockSpec(memory_space=pl.ANY)
    att = jax.ShapeDtypeStruct((1, BLK, 12 * HD), BF16)
    mix = jax.ShapeDtypeStruct((1, TOK, INNER), BF16)
    stt = jax.ShapeDtypeStruct((1, NST, TOK), BF16)
    chan = jax.ShapeDtypeStruct((1, INNER), F32)
    V = pltpu.VMEM
    D = pltpu.SemaphoreType.DMA
    scratch = [
        V((HPD, OWN, HD), BF16), V((HPD, OWN, HD), BF16), V((HPD, 2 * OWN, HD), BF16), V((HPD, 2 * OWN, HD), BF16),
        V((HPD, 2, 2 * OWN, HD), F32), V((HPD, OWN, HD), BF16),
        V((HPD, 2, OWN, HD), BF16), V((HPD, 2, OWN, HD), BF16), V((HPD, 2, OWN, HD), BF16),
        *[V((TILES, NCH * PITCH, 128), F32)] * 4,
        V((TILES, LEN, NST, NCH, 128), F32), V((TILES, NST, 128), F32),
        V((NST, LEN, NCH, 128), F32), V((NST, LEN, NCH, 128), F32), V((NCH * PITCH, 128), F32),
        V((3, NST * NCH, 128), F32),
        *[V((TILES, NCH, NST, 128), F32)] * 4,
        V((TILES, 24, 128), F32), V((NSEQ, 24, 128), F32), V((NSEQ, 16, 128), F32), V((TILES, 16, 128), F32),
        V((LEN, NST, NCH, 128), F32), V((NCH * PITCH, 128), F32), V((NCH * PITCH, 128), F32),
        V((NST, LEN * NCH, 128), F32), V((NST, LEN * NCH, 128), F32), V((NST, 128), F32),
        V((TILES, 16, 128), F32), V((NSEQ, 16, 128), F32), V((16, 128), F32), V((NGRP, 16, 128), F32),
        V((16, 128), F32), V((TILES, 16, 128), F32),
        D((4, HPD, ROW - 1)), D((4, HPD, ROW - 1)), D((4, HPD)),
        D((2, HPD)), D((2, HPD)), D((2, HPD)), D((2, HPD)),
        D((HPD, ROW - 1)), D((HPD, ROW - 1)), D((2, HPD, ROW - 1)), D((2, HPD, ROW - 1)), D((3, HPD)),
        *[D(())] * 10,
    ]
    res = pl.pallas_call(
        kernel,
        out_shape=(att, att, att, mix, mix, stt, stt, jax.ShapeDtypeStruct((NST, INNER), F32), chan, chan),
        in_specs=[hbm] * 4 + [vm] * 8,
        out_specs=(hbm,) * 3 + (vm,) * 7,
        scratch_shapes=scratch,
        compiler_params=pltpu.CompilerParams(
            collective_id=0, has_side_effects=True, vmem_limit_bytes=63 * 1024 * 1024
        ),
    )(queries, keys, values, cot_attn, x, raw, bin_, cout, cot, decay_log, step_bias.reshape(1, -1), skip_gain.reshape(1, -1))
    return tuple(res[:8]) + (res[8].reshape(-1), res[9].reshape(-1))


def solution(mesh):
    tok = P("grp", "seq", None)
    stt = P("grp", None, "seq")
    return jax.shard_map(
        per_device,
        mesh=mesh,
        in_specs=(tok,) * 4 + (tok, tok, stt, stt, tok, P(), P(), P()),
        out_specs=(tok,) * 3 + (tok, tok, stt, stt, P(), P(), P()),
        check_vma=False,
    )
```

time: 796 us -> 130 us (0.16)
  the two profiles are of different devices: /device:TPU:1 before, /device:TPU:30 now
where the time goes in v1:
time: 130 us; the launch traced here: 128 us
  Pallas kernels  117 us (90%)
  local copies, waits for them, and re-layouts  10.6 us (8%)
    pallas_call x1, Pallas kernels, per_device(): pl.pallas_call(kernel, out_shape=(att, att, att, mix, mix, stt, stt, jax....  117 us
    unnamed x28, local copies, waits for them, and re-layouts  10.6 us

profile of v1, /device:TPU:30, one launch (start us, length us, event | category | flops | bytes accessed | tf_op | source)
XLA Modules:
  0.0 128.4 jit_solution(2125854940807075197)
XLA Ops:
  0.6 117.2 %shard_map.195 = (bf16[1,256,1536]{2,1,0:T(8,128)(2,1)}, bf16[1,256,1536]{2,1,0:T(8,128)(2,1)}, bf16[1,256,1536]{2,1,0:T(8,128)(2,1)}, bf16[1,128,3072]{2,1,0:T(...) custom-call(bf16[1,256,1536]{2,1,0:T(8,128)(2,1)} %q_hbm.1, ...), custom_call_target="tpu_custom_call" | custom-call | tf_op jit(solution)/shard_map/pallas_call | solution.py:612
  117.8 0.0 copy-start.3
  117.8 2.1 %copy.32 = bf16[1,256,1536]{2,1,0:T(8,128)(2,1)} copy(bf16[1,256,1536]{2,1,0:T(8,128)(2,1)} %get-tuple-element.40) | data formatting | bytes 1572864
  120.0 0.0 copy-done.3
  120.0 0.0 copy-start.2
  120.0 0.9 copy.33
  120.9 0.5 copy-done.2
  121.4 0.0 copy-start.1
  121.4 0.9 copy.34
  122.3 0.5 copy-done.1
  122.8 0.0 copy-start
  122.8 0.9 copy.35
  123.7 0.5 copy-done
  124.2 0.9 copy.36
  125.1 0.0 copy-done.8
  125.1 0.6 copy.37
  125.7 0.1 copy-done.7
  125.8 0.6 copy.38
  126.4 0.0 copy-done.4
  126.4 0.6 copy.39
  127.0 0.1 copy-done.6
  127.1 0.6 copy.40
  127.7 0.1 copy-done.5
  127.8 0.6 copy.41
  (5 shorter events, 0.0 us)
Async XLA Ops:
  117.8 2.1 %copy-start.3 = (bf16[1,256,1536]{2,1,0:T(8,128)(2,1)S(1)}, bf16[1,256,1536]{2,1,0:T(8,128)(2,1)}, u32[]{:S(2)}) copy-start(bf16[1,256,1536]{2,1,0:T(8,128)(2,1)} %get-tuple-element.41) | copy-start | bytes 2359300
  120.0 1.4 %copy-start.2 = (bf16[1,256,1536]{2,1,0:T(8,128)(2,1)S(1)}, bf16[1,256,1536]{2,1,0:T(8,128)(2,1)}, u32[]{:S(2)}) copy-start(bf16[1,256,1536]{2,1,0:T(8,128)(2,1)} %get-tuple-element.42) | copy-start | bytes 2359300
  121.4 1.4 %copy-start.1 = (bf16[1,128,3072]{2,1,0:T(8,128)(2,1)S(1)}, bf16[1,128,3072]{2,1,0:T(8,128)(2,1)}, u32[]{:S(2)}) copy-start(bf16[1,128,3072]{2,1,0:T(8,128)(2,1)} %get-tuple-element.43) | copy-start | bytes 2359300
  122.8 1.4 %copy-start = (bf16[1,128,3072]{2,1,0:T(8,128)(2,1)S(1)}, bf16[1,128,3072]{2,1,0:T(8,128)(2,1)}, u32[]{:S(2)}) copy-start(bf16[1,128,3072]{2,1,0:T(8,128)(2,1)} %get-tuple-element.44) | copy-start | bytes 2359300
  124.2 0.9 copy-start.8
  124.2 2.1 %copy-start.4 = (f32[8,3072]{1,0:T(8,128)S(1)}, f32[8,3072]{1,0:T(8,128)}, u32[]{:S(2)}) copy-start(f32[8,3072]{1,0:T(8,128)} %get-tuple-element.47) | copy-start | bytes 294916
  125.1 0.7 copy-start.7
  126.4 0.7 copy-start.6
  127.1 0.7 copy-start.5

commit v2 on v1

--- a/solution.py
+++ b/solution.py
@@ -46,7 +46,7 @@
     qs, dos, ks, vs, acc, qout, retout, retin, fin,
     dts, xs, cts, sgs, avs, a2s, btab, ctab, natt, tscr, pds, pes, sds, sbs, tot, gath, cbuf, cin,
     ahs, gxt, grt, gbacc, gcacc, gred, par, pgat, psm, p4, pfin, pout,
-    in_send, in_recv, in_loc, fw_send, fw_recv, rt_send, rt_recv, q_send, q_recv, o_send, o_recv, o_loc,
+    in_send, in_recv, in_loc, fw_send, fw_recv, rt_send, rt_recv, o_send, o_recv, o_loc,
     a_send, a_recv, b_send, b_recv, c_send, c_recv, d_send, d_recv, e_send, e_recv,
 ):
     s = lax.axis_index("seq")
@@ -110,84 +110,107 @@
             srcs[t].at[0, :, lanes], dsts[t].at[h, rows, :], in_loc.at[t, h]
         )
 
-    def send_in(h):
-        for t in range(4):
-            for off in range(1, ROW):
-                in_copy(t, h, off).start()
-            in_local(t, h).start()
-
-    def fw_copy(t, h):
+    def send_in(t, h):
+        for off in range(1, ROW):
+            in_copy(t, h, off).start()
+        in_local(t, h).start()
+
+    def block_rows(start, j):
+        return pl.ds(pl.multiple_of(start + j * BLK, BLK), BLK)
+
+    def fw_copy(t, h, j, own=False):
+        lanes = pl.ds(pl.multiple_of((col * HPD + h) * HD, HD), HD)
         return pltpu.make_async_remote_copy(
-            src_ref=dsts[t].at[h, pl.ds(OWN, OWN), :],
-            dst_ref=dsts[t].at[h, pl.ds(0, OWN), :],
-            send_sem=fw_send.at[t, h],
-            recv_sem=fw_recv.at[t, h],
+            src_ref=srcs[t].at[0, :, lanes] if own else dsts[t].at[h, block_rows(OWN, j), :],
+            dst_ref=dsts[t].at[h, block_rows(0, j), :],
+            send_sem=fw_send.at[t, h, j],
+            recv_sem=fw_recv.at[t, h, j],
             device_id={"seq": lax.rem(s + ROW, NSEQ)},
             device_id_type=MESH,
         )
 
-    def forward_kv(h):
-        for t in range(2):
-            for off in range(1, ROW):
+    def forward_own(h):
+        @pl.when(jnp.logical_not(last))
+        def _():
+            for t in range(2):
+                fw_copy(t, h, col, own=True).start()
+
+    def forward_rest(h):
+        for off in range(1, ROW):
+            for t in range(2):
                 in_wait(t, h, off)
-            in_local(t, h).wait()
 
             @pl.when(jnp.logical_not(last))
             def _():
-                fw_copy(t, h).start()
-
-    def rt_copy(t, h):
+                for t in range(2):
+                    fw_copy(t, h, lax.rem(col + ROW - off, ROW)).start()
+
+    def rt_copy(t, h, j):
         return pltpu.make_async_remote_copy(
-            src_ref=retout.at[h, t],
-            dst_ref=retin.at[h, t],
-            send_sem=rt_send.at[t, h],
-            recv_sem=rt_recv.at[t, h],
+            src_ref=retout.at[h, t, block_rows(0, j), :],
+            dst_ref=retin.at[h, t, block_rows(0, j), :],
+            send_sem=rt_send.at[t, h, j],
+            recv_sem=rt_recv.at[t, h, j],
             device_id={"seq": lax.rem(s + NSEQ - ROW, NSEQ)},
             device_id_type=MESH,
         )
 
-    outs = (dk_hbm, dv_hbm)
-
-    def out_copy(src, dst, h, off, send, recv):
-        peer = lax.rem(col + off, ROW)
+    outs = (dk_hbm, dv_hbm, dq_hbm)
+
+    def out_src(t, h):
+        return qout.at[h] if t == 2 else fin.at[h, t]
+
+    def out_remote(t, h, j):
         lanes = pl.ds(pl.multiple_of((col * HPD + h) * HD, HD), HD)
-        rows = pl.ds(pl.multiple_of(peer * BLK, BLK), BLK)
         return pltpu.make_async_remote_copy(
-            src_ref=src.at[rows, :],
-            dst_ref=dst.at[0, :, lanes],
-            send_sem=send,
-            recv_sem=recv,
-            device_id={"seq": base + peer},
+            src_ref=out_src(t, h).at[block_rows(0, j), :],
+            dst_ref=outs[t].at[0, :, lanes],
+            send_sem=o_send.at[t, h, j],
+            recv_sem=o_recv.at[t, h, col],
+            device_id={"seq": base + j},
             device_id_type=MESH,
         )
 
-    def out_wait(src, dst, h, off, send, recv):
-        peer = lax.rem(col + ROW - off, ROW)
+    def out_local(t, h):
+        lanes = pl.ds(pl.multiple_of((col * HPD + h) * HD, HD), HD)
+        return pltpu.make_async_copy(
+            out_src(t, h).at[block_rows(0, col), :], outs[t].at[0, :, lanes], o_loc.at[t, h]
+        )
+
+    def out_wait(t, h, peer):
         lanes = pl.ds(pl.multiple_of((peer * HPD + h) * HD, HD), HD)
         pltpu.make_async_remote_copy(
-            src_ref=src.at[pl.ds(0, BLK), :],
-            dst_ref=dst.at[0, :, lanes],
-            send_sem=send,
-            recv_sem=recv,
+            src_ref=out_src(t, h).at[block_rows(0, col), :],
+            dst_ref=outs[t].at[0, :, lanes],
+            send_sem=o_send.at[t, h, peer],
+            recv_sem=o_recv.at[t, h, peer],
             device_id={"seq": base + peer},
             device_id_type=MESH,
         ).wait_recv()
 
-    def out_local(src, dst, h, sem):
-        lanes = pl.ds(pl.multiple_of((col * HPD + h) * HD, HD), HD)
-        rows = pl.ds(pl.multiple_of(col * BLK, BLK), BLK)
-        return pltpu.make_async_copy(src.at[rows, :], dst.at[0, :, lanes], sem)
-
-    def attention(h):
+    def out_start(ts, h, j):
+        @pl.when(j == col)
+        def _():
+            for t in ts:
+                out_local(t, h).start()
+
+        @pl.when(j != col)
+        def _():
+            for t in ts:
+                out_remote(t, h, j).start()
+
+    def attention(h, hooks):
+        for t in range(4):
+            in_local(t, h).wait()
         for t in range(2, 4):
             for off in range(1, ROW):
                 in_wait(t, h, off)
-            in_local(t, h).wait()
 
         @pl.when(jnp.logical_not(first))
         def _():
-            for t in range(2):
-                fw_copy(t, h).wait_recv()
+            for j in range(ROW):
+                for t in range(2):
+                    fw_copy(t, h, j).wait_recv()
 
         @pl.when(first)
         def _():
@@ -202,6 +225,7 @@
 
         @pl.loop(0, ROW)
         def _(i):
+            run_hooks(hooks, i)
             at = pl.multiple_of(i * BLK, BLK)
             qrows = pl.ds(at, BLK)
             krows = pl.ds(at, OWN + BLK)
@@ -239,34 +263,34 @@
             dq = dot(kb, dfull, TN)
             qout[h, qrows, :] = (dq.T * SCALE).astype(BF16)
 
-        for off in range(1, ROW):
-            out_copy(qout.at[h], dq_hbm, h, off, q_send.at[h, off - 1], q_recv.at[h, off - 1]).start()
-        out_local(qout.at[h], dq_hbm, h, o_loc.at[2, h]).start()
-
-        @pl.when(jnp.logical_not(first))
-        def _():
-            retout[h, 0] = (acc[h, 0, pl.ds(0, OWN), :] * SCALE).astype(BF16)
-            rt_copy(0, h).start()
-            retout[h, 1] = acc[h, 1, pl.ds(0, OWN), :].astype(BF16)
-            rt_copy(1, h).start()
+            out_start((2,), h, i)
+
+            @pl.when(jnp.logical_not(first))
+            def _():
+                retout[h, 0, qrows, :] = (acc[h, 0, qrows, :] * SCALE).astype(BF16)
+                retout[h, 1, qrows, :] = acc[h, 1, qrows, :].astype(BF16)
+                for t in range(2):
+                    rt_copy(t, h, i).start()
 
     def finish_head(h):
-        for t in range(2):
-            scale = SCALE if t == 0 else 1.0
-
-            @pl.when(last)
-            def _():
-                fin[h, t] = (acc[h, t, pl.ds(OWN, OWN), :] * scale).astype(BF16)
-
-            @pl.when(jnp.logical_not(last))
-            def _():
-                rt_copy(t, h).wait_recv()
-                own = acc[h, t, pl.ds(OWN, OWN), :] * scale
-                fin[h, t] = (own + retin[h, t].astype(F32)).astype(BF16)
-
-            for off in range(1, ROW):
-                out_copy(fin.at[h, t], outs[t], h, off, o_send.at[t, h, off - 1], o_recv.at[t, h, off - 1]).start()
-            out_local(fin.at[h, t], outs[t], h, o_loc.at[t, h]).start()
+        @pl.loop(0, ROW)
+        def _(j):
+            rows = block_rows(0, j)
+            own = block_rows(OWN, j)
+            for t in range(2):
+                scale = SCALE if t == 0 else 1.0
+
+                @pl.when(last)
+                def _():
+                    fin[h, t, rows, :] = (acc[h, t, own, :] * scale).astype(BF16)
+
+                @pl.when(jnp.logical_not(last))
+                def _():
+                    rt_copy(t, h, j).wait_recv()
+                    mine = acc[h, t, own, :] * scale
+                    fin[h, t, rows, :] = (mine + retin[h, t, rows, :].astype(F32)).astype(BF16)
+
+            out_start((0, 1), h, j)
 
     def drain():
         @pl.loop(0, HPD)
@@ -274,25 +298,29 @@
             for t in range(4):
                 for off in range(1, ROW):
                     in_copy(t, h, off).wait_send()
-            for off in range(1, ROW):
-                out_copy(qout.at[h], dq_hbm, h, off, q_send.at[h, off - 1], q_recv.at[h, off - 1]).wait_send()
-                out_wait(qout.at[h], dq_hbm, h, off, q_send.at[h, off - 1], q_recv.at[h, off - 1])
-            out_local(qout.at[h], dq_hbm, h, o_loc.at[2, h]).wait()
-            for t in range(2):
-
-                @pl.when(jnp.logical_not(last))
+
+            @pl.loop(0, ROW)
+            def _(j):
+                for t in range(2):
+
+                    @pl.when(jnp.logical_not(last))
+                    def _():
+                        fw_copy(t, h, j).wait_send()
+
+                    @pl.when(jnp.logical_not(first))
+                    def _():
+                        rt_copy(t, h, j).wait_send()
+
+                @pl.when(j == col)
                 def _():
-                    fw_copy(t, h).wait_send()
-
-                @pl.when(jnp.logical_not(first))
+                    for t in range(3):
+                        out_local(t, h).wait()
+
+                @pl.when(j != col)
                 def _():
-                    rt_copy(t, h).wait_send()
-
-                for off in range(1, ROW):
-                    sems = (o_send.at[t, h, off - 1], o_recv.at[t, h, off - 1])
-                    out_copy(fin.at[h, t], outs[t], h, off, *sems).wait_send()
-                    out_wait(fin.at[h, t], outs[t], h, off, *sems)
-                out_local(fin.at[h, t], outs[t], h, o_loc.at[t, h]).wait()
+                    for t in range(3):
+                        out_remote(t, h, j).wait_send()
+                        out_wait(t, h, j)
 
     def mixer_tables():
         bin32 = bin_ref[0].astype(F32)
@@ -543,42 +571,66 @@
             part = pgat.at[pl.ds(0, NSEQ - 1)]
             pltpu.make_async_copy(part, part, e_send).wait()
 
-    send_in(0)
+    def run_hooks(hooks, i):
+        for at, action in hooks:
+
+            @pl.when(i == at)
+            def _():
+                action()
+
+    def tiles(body, start, stop, hooks):
+        @pl.loop(start, stop)
+        def _(c):
+            run_hooks(hooks, c)
+            body(c)
+
+    K, VV, Q, DO = range(4)
+
+    def send(*pairs):
+        def go():
+            for t, h in pairs:
+                send_in(t, h)
+
+        return go
+
+    send((K, 0), (VV, 0))()
+    for h in range(HPD):
+        forward_own(h)
     mixer_tables()
-
-    @pl.loop(0, TILES)
-    def _(c):
-        mixer_local(c)
-
+    tiles(mixer_local, 0, TILES, [(4, send((Q, 0))), (16, lambda: forward_rest(0))])
     scatter(tot, gath, a_send, a_recv)
-    send_in(1)
-    send_in(2)
-    forward_kv(0)
-    mixer_prefix()
+    send((DO, 0), (K, 1), (VV, 1))()
     gbacc[...] = jnp.zeros(gbacc.shape, F32)
     gcacc[...] = jnp.zeros(gcacc.shape, F32)
     par[:, 10:16, :] = jnp.zeros((TILES, 6, 128), F32)
-    forward_kv(1)
+    mixer_prefix()
+    send((Q, 1), (DO, 1))()
+    attention(0, [(2, lambda: forward_rest(1)), (3, send((K, 2), (VV, 2)))])
     tiles_wait(cin, b_recv)
-
-    @pl.loop(0, TILES)
-    def _(c):
-        mixer_back(c)
-
+    tiles(mixer_back, 0, TILES // 2, [(1, send((Q, 2), (DO, 2))), (TILES // 2 - 3, lambda: forward_rest(2))])
+    attention(1, [])
+    finish_head(0)
+    tiles(mixer_back, TILES // 2, TILES, [])
     scatter(par, pgat, c_send, c_recv)
-    forward_kv(2)
+    attention(2, [])
+    params_rows()
     mixer_state_grads()
-    params_rows()
-    attention(0)
+    finish_head(1)
     params_groups()
-    attention(1)
-    finish_head(0)
+    finish_head(2)
     params_store()
-    attention(2)
-    finish_head(1)
     mixer_drain()
-    finish_head(2)
     drain()
+
+
+def store_results(*refs):
+    n = len(refs) // 2
+    srcs, outs, sems = refs[:n], refs[n : 2 * n], refs[2 * n]
+    copies = [pltpu.make_async_copy(a, b, sems.at[i]) for i, (a, b) in enumerate(zip(srcs, outs))]
+    for copy in copies:
+        copy.start()
+    for copy in copies:
+        copy.wait()
 
 
 def per_device(queries, keys, values, cot_attn, x, raw, bin_, cout, cot, decay_log, step_bias, skip_gain):
@@ -589,6 +641,7 @@
     stt = jax.ShapeDtypeStruct((1, NST, TOK), BF16)
     chan = jax.ShapeDtypeStruct((1, INNER), F32)
     V = pltpu.VMEM
+    shapes = (att, att, att, mix, mix, stt, stt, jax.ShapeDtypeStruct((NST, INNER), F32), chan, chan)
     D = pltpu.SemaphoreType.DMA
     scratch = [
         V((HPD, OWN, HD), BF16), V((HPD, OWN, HD), BF16), V((HPD, 2 * OWN, HD), BF16), V((HPD, 2 * OWN, HD), BF16),
@@ -605,20 +658,28 @@
         V((TILES, 16, 128), F32), V((NSEQ, 16, 128), F32), V((16, 128), F32), V((NGRP, 16, 128), F32),
         V((16, 128), F32), V((TILES, 16, 128), F32),
         D((4, HPD, ROW - 1)), D((4, HPD, ROW - 1)), D((4, HPD)),
-        D((2, HPD)), D((2, HPD)), D((2, HPD)), D((2, HPD)),
-        D((HPD, ROW - 1)), D((HPD, ROW - 1)), D((2, HPD, ROW - 1)), D((2, HPD, ROW - 1)), D((3, HPD)),
+        *[D((2, HPD, ROW))] * 4,
+        D((3, HPD, ROW)), D((3, HPD, ROW)), D((3, HPD)),
         *[D(())] * 10,
     ]
     res = pl.pallas_call(
         kernel,
-        out_shape=(att, att, att, mix, mix, stt, stt, jax.ShapeDtypeStruct((NST, INNER), F32), chan, chan),
+        out_shape=tuple(V(a.shape, a.dtype) for a in shapes),
         in_specs=[hbm] * 4 + [vm] * 8,
-        out_specs=(hbm,) * 3 + (vm,) * 7,
+        out_specs=(vm,) * 10,
         scratch_shapes=scratch,
         compiler_params=pltpu.CompilerParams(
-            collective_id=0, has_side_effects=True, vmem_limit_bytes=63 * 1024 * 1024
+            collective_id=0, has_side_effects=True, vmem_limit_bytes=56 * 1024 * 1024
         ),
     )(queries, keys, values, cot_attn, x, raw, bin_, cout, cot, decay_log, step_bias.reshape(1, -1), skip_gain.reshape(1, -1))
+    res = pl.pallas_call(
+        store_results,
+        out_shape=shapes,
+        in_specs=[vm] * len(shapes),
+        out_specs=(hbm,) * len(shapes),
+        scratch_shapes=[D((len(shapes),))],
+        compiler_params=pltpu.CompilerParams(vmem_limit_bytes=4 * 1024 * 1024),
+    )(*[pltpu.with_memory_space_constraint(a, pltpu.VMEM) for a in res])
     return tuple(res[:8]) + (res[8].reshape(-1), res[9].reshape(-1))
 
 

time: 130 us -> 100 us (0.77); the launches traced: 128 us -> 100 us
  Pallas kernels: 117 us -> 99.5 us
  local copies, waits for them, and re-layouts: 10.6 us -> 0 us
    pallas_call x1 -> x2, Pallas kernels: 117 us -> 99.5 us  [the longest x1 97.4 us: per_device(): pl.pallas_call(kernel, out_shape=tuple((V(a.shape, a.dtype) for a in shap...]
    unnamed x28 -> x0, local copies, waits for them, and re-layouts: 10.6 us -> none
where the time goes in v2:
time: 100 us
  Pallas kernels  99.5 us (100%)
    pallas_call x1, Pallas kernels, per_device(): pl.pallas_call(kernel, out_shape=tuple((V(a.shape, a.dtype) for a in shap...  97.4 us
    pallas_call x1, Pallas kernels, per_device(): pl.pallas_call(store_results, out_shape=shapes, in_specs=[vm] * len(shape...  2.04 us

profile of v2, /device:TPU:30, one launch (start us, length us, event | category | flops | bytes accessed | tf_op | source)
XLA Modules:
  0.0 100.1 jit_solution(15556063249776427460)
XLA Ops:
  0.6 97.4 %shard_map.195 = (bf16[1,256,1536]{2,1,0:T(8,128)(2,1)S(1)}, bf16[1,256,1536]{2,1,0:T(8,128)(2,1)S(1)}, bf16[1,256,1536]{2,1,0:T(8,128)(2,1)S(1)}, bf16[1,128,30...) custom-call(bf16[1,256,1536]{2,1,0:T(8,128)(2,1)} %q_hbm.1, ...), custom_call_target="tpu_custom_call" | custom-call | tf_op jit(solution)/shard_map/pallas_call | solution.py:665
  98.1 2.0 %shard_map.196 = (bf16[1,256,1536]{2,1,0:T(8,128)(2,1)}, bf16[1,256,1536]{2,1,0:T(8,128)(2,1)}, bf16[1,256,1536]{2,1,0:T(8,128)(2,1)}, bf16[1,128,3072]{2,1,0:T(...) custom-call(bf16[1,256,1536]{2,1,0:T(8,128)(2,1)S(1)} %get-tuple-ele, ...), custom_call_target="tpu_custom_call" | custom-call | tf_op jit(solution)/shard_map/pallas_call | solution.py:675

commit v3 on v2

--- a/solution.py
+++ b/solution.py
@@ -41,13 +41,13 @@
 
 
 def kernel(
-    q_hbm, k_hbm, v_hbm, do_hbm, x_ref, raw_ref, bin_ref, cout_ref, cot_ref, dl_ref, bias_ref, skip_ref,
+    q_hbm, k_hbm, v_hbm, do_hbm, x_hbm, raw_hbm, bin_ref, cout_ref, cot_hbm, dl_ref, bias_ref, skip_ref,
     dq_hbm, dk_hbm, dv_hbm, gx_ref, gr_ref, gin_ref, gout_ref, gdec_ref, gbias_ref, gskip_ref,
     qs, dos, ks, vs, acc, qout, retout, retin, fin,
-    dts, xs, cts, sgs, avs, a2s, btab, ctab, natt, tscr, pds, pes, sds, sbs, tot, gath, cbuf, cin,
+    x_ref, raw_ref, cot_ref, mix_sem, dts, xs, cts, sgs, avs, a2s, btab, ctab, natt, tscr, pds, pes, sds, sbs, tot, dtot, gath, gdt, ahead, cbuf, cin,
     ahs, gxt, grt, gbacc, gcacc, gred, par, pgat, psm, p4, pfin, pout,
     in_send, in_recv, in_loc, fw_send, fw_recv, rt_send, rt_recv, o_send, o_recv, o_loc,
-    a_send, a_recv, b_send, b_recv, c_send, c_recv, d_send, d_recv, e_send, e_recv,
+    a_send, a_recv, t_send, t_recv, b_send, b_recv, c_send, c_recv, d_send, d_recv, e_send, e_recv,
 ):
     s = lax.axis_index("seq")
     g = lax.axis_index("grp")
@@ -56,6 +56,13 @@
     row = s // ROW
     first = row == 0
     last = row == NROW - 1
+
+    mix_in = [
+        pltpu.make_async_copy(src, dst, mix_sem.at[i])
+        for i, (src, dst) in enumerate(((x_hbm, x_ref), (raw_hbm, raw_ref), (cot_hbm, cot_ref)))
+    ]
+    for copy in mix_in:
+        copy.start()
 
     barrier = pltpu.get_barrier_semaphore()
 
@@ -391,9 +398,8 @@
             sbs[c, k] = sb
             sb = dk[k] * sb + bk[k]
             sd = dk[k] * sd
-        tot[c, 0:8, :] = pe
-        tot[c, 8:16, :] = pd
-        tot[c, 16:24, :] = sb
+        tot[c] = jnp.concatenate([pe, sb], 0).astype(BF16)
+        dtot[c] = jnp.sum(dt, axis=0, keepdims=True)
 
     def scatter(src, dst, send, recv):
         @pl.loop(0, TILES)
@@ -438,21 +444,24 @@
         @pl.when(s < TILES)
         def _():
             scatter_wait_recv(gath, a_recv)
+            scatter_wait_recv(gdt, t_recv)
+            a2 = a2s[s]
             carry = jnp.zeros((NST, 128), F32)
             for i in range(NSEQ):
-                cbuf[i, 0:8, :] = carry
-                carry = gath[i, 8:16, :] * carry + gath[i, 0:8, :]
+                ahead[i] = carry
+                carry = jnp.exp2(a2 * gdt[i]) * carry + gath[i].astype(F32)[0:8]
             carry = jnp.zeros((NST, 128), F32)
             for i in reversed(range(NSEQ)):
-                cbuf[i, 8:16, :] = carry
-                carry = gath[i, 8:16, :] * carry + gath[i, 16:24, :]
+                cbuf[i] = jnp.concatenate([ahead[i], carry], 0).astype(BF16)
+                carry = jnp.exp2(a2 * gdt[i]) * carry + gath[i].astype(F32)[8:16]
             spread_out(lambda i: cbuf.at[i], cin, b_send, b_recv)
             cin[s] = cbuf[s]
 
     def mixer_back(c):
         lanes = pl.ds(pl.multiple_of(c * 128, 128), 128)
-        hin = cin[c, 0:8, :]
-        gin = cin[c, 8:16, :]
+        entering = cin[c].astype(F32)
+        hin = entering[0:8]
+        gin = entering[8:16]
         for k in range(NCH):
             rows = pl.ds(k * NST, NST)
             tscr[0, rows, :] = pds[c, k] * hin + pes[c, k]
@@ -560,6 +569,7 @@
 
     def mixer_drain():
         tiles_wait(tot, a_send)
+        tiles_wait(dtot, t_send)
         tiles_wait(par, c_send)
 
         @pl.when(s < TILES)
@@ -597,26 +607,29 @@
     for h in range(HPD):
         forward_own(h)
     mixer_tables()
-    tiles(mixer_local, 0, TILES, [(4, send((Q, 0))), (16, lambda: forward_rest(0))])
+    for copy in mix_in:
+        copy.wait()
+    tiles(mixer_local, 0, TILES, [(4, send((Q, 0)))])
     scatter(tot, gath, a_send, a_recv)
-    send((DO, 0), (K, 1), (VV, 1))()
+    scatter(dtot, gdt, t_send, t_recv)
+    send((DO, 0))()
     gbacc[...] = jnp.zeros(gbacc.shape, F32)
     gcacc[...] = jnp.zeros(gcacc.shape, F32)
-    par[:, 10:16, :] = jnp.zeros((TILES, 6, 128), F32)
     mixer_prefix()
-    send((Q, 1), (DO, 1))()
-    attention(0, [(2, lambda: forward_rest(1)), (3, send((K, 2), (VV, 2)))])
+    forward_rest(0)
+    send((K, 1), (VV, 1), (K, 2), (VV, 2), (Q, 1), (DO, 1), (Q, 2), (DO, 2))()
     tiles_wait(cin, b_recv)
-    tiles(mixer_back, 0, TILES // 2, [(1, send((Q, 2), (DO, 2))), (TILES // 2 - 3, lambda: forward_rest(2))])
+    tiles(mixer_back, 0, TILES // 2, [(9, lambda: forward_rest(1))])
+    attention(0, [(2, lambda: forward_rest(2))])
+    tiles(mixer_back, TILES // 2, TILES, [])
+    scatter(par, pgat, c_send, c_recv)
+    mixer_state_grads()
     attention(1, [])
     finish_head(0)
-    tiles(mixer_back, TILES // 2, TILES, [])
-    scatter(par, pgat, c_send, c_recv)
+    params_rows()
     attention(2, [])
-    params_rows()
-    mixer_state_grads()
+    params_groups()
     finish_head(1)
-    params_groups()
     finish_head(2)
     params_store()
     mixer_drain()
@@ -647,25 +660,27 @@
         V((HPD, OWN, HD), BF16), V((HPD, OWN, HD), BF16), V((HPD, 2 * OWN, HD), BF16), V((HPD, 2 * OWN, HD), BF16),
         V((HPD, 2, 2 * OWN, HD), F32), V((HPD, OWN, HD), BF16),
         V((HPD, 2, OWN, HD), BF16), V((HPD, 2, OWN, HD), BF16), V((HPD, 2, OWN, HD), BF16),
+        *[V((1, TOK, INNER), BF16)] * 3, D((3,)),
         *[V((TILES, NCH * PITCH, 128), F32)] * 4,
         V((TILES, LEN, NST, NCH, 128), F32), V((TILES, NST, 128), F32),
         V((NST, LEN, NCH, 128), F32), V((NST, LEN, NCH, 128), F32), V((NCH * PITCH, 128), F32),
         V((3, NST * NCH, 128), F32),
         *[V((TILES, NCH, NST, 128), F32)] * 4,
-        V((TILES, 24, 128), F32), V((NSEQ, 24, 128), F32), V((NSEQ, 16, 128), F32), V((TILES, 16, 128), F32),
+        V((TILES, 16, 128), BF16), V((TILES, 1, 128), F32), V((NSEQ, 16, 128), BF16), V((NSEQ, 1, 128), F32),
+        V((NSEQ, NST, 128), F32), V((NSEQ, 16, 128), BF16), V((TILES, 16, 128), BF16),
         V((LEN, NST, NCH, 128), F32), V((NCH * PITCH, 128), F32), V((NCH * PITCH, 128), F32),
         V((NST, LEN * NCH, 128), F32), V((NST, LEN * NCH, 128), F32), V((NST, 128), F32),
-        V((TILES, 16, 128), F32), V((NSEQ, 16, 128), F32), V((16, 128), F32), V((NGRP, 16, 128), F32),
-        V((16, 128), F32), V((TILES, 16, 128), F32),
+        V((TILES, 10, 128), F32), V((NSEQ, 10, 128), F32), V((10, 128), F32), V((NGRP, 10, 128), F32),
+        V((10, 128), F32), V((TILES, 10, 128), F32),
         D((4, HPD, ROW - 1)), D((4, HPD, ROW - 1)), D((4, HPD)),
         *[D((2, HPD, ROW))] * 4,
         D((3, HPD, ROW)), D((3, HPD, ROW)), D((3, HPD)),
-        *[D(())] * 10,
+        *[D(())] * 12,
     ]
     res = pl.pallas_call(
         kernel,
         out_shape=tuple(V(a.shape, a.dtype) for a in shapes),
-        in_specs=[hbm] * 4 + [vm] * 8,
+        in_specs=[hbm] * 6 + [vm] * 2 + [hbm] + [vm] * 3,
         out_specs=(vm,) * 10,
         scratch_shapes=scratch,
         compiler_params=pltpu.CompilerParams(

time: 100 us -> 83.9 us (0.84)
  Pallas kernels: 99.5 us -> 83.1 us
    pallas_call x1, Pallas kernels: 97.4 us -> 81 us  [per_device(): pl.pallas_call(kernel, out_shape=tuple((V(a.shape, a.dtype) for a in shap...]
where the time goes in v3:
time: 83.9 us; the launch traced here: 83.7 us
  Pallas kernels  83.1 us (99%)
    pallas_call x1, Pallas kernels, per_device(): pl.pallas_call(kernel, out_shape=tuple((V(a.shape, a.dtype) for a in shap...  81 us
    pallas_call x1, Pallas kernels, per_device(): pl.pallas_call(store_results, out_shape=shapes, in_specs=[vm] * len(shape...  2.04 us

profile of v3, /device:TPU:30, one launch (start us, length us, event | category | flops | bytes accessed | tf_op | source)
XLA Modules:
  0.0 83.7 jit_solution(1156977291589492237)
XLA Ops:
  0.6 81.0 %shard_map.195 = (bf16[1,256,1536]{2,1,0:T(8,128)(2,1)S(1)}, bf16[1,256,1536]{2,1,0:T(8,128)(2,1)S(1)}, bf16[1,256,1536]{2,1,0:T(8,128)(2,1)S(1)}, bf16[1,128,30...) custom-call(bf16[1,256,1536]{2,1,0:T(8,128)(2,1)} %q_hbm.1, ...), custom_call_target="tpu_custom_call" | custom-call | tf_op jit(solution)/shard_map/pallas_call | solution.py:680
  81.7 2.0 %shard_map.196 = (bf16[1,256,1536]{2,1,0:T(8,128)(2,1)}, bf16[1,256,1536]{2,1,0:T(8,128)(2,1)}, bf16[1,256,1536]{2,1,0:T(8,128)(2,1)}, bf16[1,128,3072]{2,1,0:T(...) custom-call(bf16[1,256,1536]{2,1,0:T(8,128)(2,1)S(1)} %get-tuple-ele, ...), custom_call_target="tpu_custom_call" | custom-call | tf_op jit(solution)/shard_map/pallas_call | solution.py:690

commit v4 on v3

--- a/solution.py
+++ b/solution.py
@@ -31,6 +31,8 @@
 NEG = -1e30
 SCALE = HD**-0.5
 
+AWAY = (2, 1, 3, 0)
+
 NT = (((1,), (1,)), ((), ()))
 NN = (((1,), (0,)), ((), ()))
 TN = (((0,), (0,)), ((), ()))
@@ -206,7 +208,7 @@
             for t in ts:
                 out_remote(t, h, j).start()
 
-    def attention(h, hooks):
+    def attention(h, hooks, at_once=True):
         for t in range(4):
             in_local(t, h).wait()
         for t in range(2, 4):
@@ -276,12 +278,21 @@
             def _():
                 retout[h, 0, qrows, :] = (acc[h, 0, qrows, :] * SCALE).astype(BF16)
                 retout[h, 1, qrows, :] = acc[h, 1, qrows, :].astype(BF16)
-                for t in range(2):
-                    rt_copy(t, h, i).start()
+                if at_once:
+                    for t in range(2):
+                        rt_copy(t, h, i).start()
+
+        if not at_once:
+
+            @pl.when(jnp.logical_not(first))
+            def _():
+                for off in AWAY:
+                    for t in range(2):
+                        rt_copy(t, h, lax.rem(col + off, ROW)).start()
 
     def finish_head(h):
-        @pl.loop(0, ROW)
-        def _(j):
+        for off in AWAY:
+            j = lax.rem(col + off, ROW)
             rows = block_rows(0, j)
             own = block_rows(OWN, j)
             for t in range(2):
@@ -627,9 +638,9 @@
     attention(1, [])
     finish_head(0)
     params_rows()
-    attention(2, [])
+    attention(2, [], at_once=False)
+    finish_head(1)
     params_groups()
-    finish_head(1)
     finish_head(2)
     params_store()
     mixer_drain()

time: 83.9 us -> 82.2 us (0.980)
  Pallas kernels: 83.1 us -> 80.7 us
    pallas_call x1, Pallas kernels: 81 us -> 78.7 us  [per_device(): pl.pallas_call(kernel, out_shape=tuple((V(a.shape, a.dtype) for a in shap...]
where the time goes in v4:
time: 82.2 us; the launch traced here: 81.4 us
  Pallas kernels  80.7 us (98%)
    pallas_call x1, Pallas kernels, per_device(): pl.pallas_call(kernel, out_shape=tuple((V(a.shape, a.dtype) for a in shap...  78.7 us
    pallas_call x1, Pallas kernels, per_device(): pl.pallas_call(store_results, out_shape=shapes, in_specs=[vm] * len(shape...  2.04 us

profile of v4, /device:TPU:30, one launch (start us, length us, event | category | flops | bytes accessed | tf_op | source)
XLA Modules:
  0.0 81.4 jit_solution(3721413635140775568)
XLA Ops:
  0.6 78.7 %shard_map.195 = (bf16[1,256,1536]{2,1,0:T(8,128)(2,1)S(1)}, bf16[1,256,1536]{2,1,0:T(8,128)(2,1)S(1)}, bf16[1,256,1536]{2,1,0:T(8,128)(2,1)S(1)}, bf16[1,128,30...) custom-call(bf16[1,256,1536]{2,1,0:T(8,128)(2,1)} %q_hbm.1, ...), custom_call_target="tpu_custom_call" | custom-call | tf_op jit(solution)/shard_map/pallas_call | solution.py:691
  79.3 2.0 %shard_map.196 = (bf16[1,256,1536]{2,1,0:T(8,128)(2,1)}, bf16[1,256,1536]{2,1,0:T(8,128)(2,1)}, bf16[1,256,1536]{2,1,0:T(8,128)(2,1)}, bf16[1,128,3072]{2,1,0:T(...) custom-call(bf16[1,256,1536]{2,1,0:T(8,128)(2,1)S(1)} %get-tuple-ele, ...), custom_call_target="tpu_custom_call" | custom-call | tf_op jit(solution)/shard_map/pallas_call | solution.py:701

commit v5 on v4

--- a/solution.py
+++ b/solution.py
@@ -43,12 +43,12 @@
 
 
 def kernel(
-    q_hbm, k_hbm, v_hbm, do_hbm, x_hbm, raw_hbm, bin_ref, cout_ref, cot_hbm, dl_ref, bias_ref, skip_ref,
+    q_hbm, k_hbm, v_hbm, do_hbm, x_hbm, raw_hbm, bin_hbm, cout_hbm, cot_hbm, dl_hbm, bias_hbm, skip_hbm,
     dq_hbm, dk_hbm, dv_hbm, gx_ref, gr_ref, gin_ref, gout_ref, gdec_ref, gbias_ref, gskip_ref,
     qs, dos, ks, vs, acc, qout, retout, retin, fin,
-    x_ref, raw_ref, cot_ref, mix_sem, dts, xs, cts, sgs, avs, a2s, btab, ctab, natt, tscr, pds, pes, sds, sbs, tot, dtot, gath, gdt, ahead, cbuf, cin,
+    x_ref, raw_ref, cot_ref, bin_ref, cout_ref, dl_ref, bias_ref, skip_ref, mix_sem, dts, xs, cts, sgs, avs, a2s, btab, ctab, natt, tscr, pds, pes, sds, sbs, tot, dtot, gath, gdt, ahead, cbuf, cin,
     ahs, gxt, grt, gbacc, gcacc, gred, par, pgat, psm, p4, pfin, pout,
-    in_send, in_recv, in_loc, fw_send, fw_recv, rt_send, rt_recv, o_send, o_recv, o_loc,
+    heard, in_send, in_recv, in_loc, fw_send, fw_recv, rt_send, rt_recv, o_send, o_recv, o_loc,
     a_send, a_recv, t_send, t_recv, b_send, b_recv, c_send, c_recv, d_send, d_recv, e_send, e_recv,
 ):
     s = lax.axis_index("seq")
@@ -61,26 +61,36 @@
 
     mix_in = [
         pltpu.make_async_copy(src, dst, mix_sem.at[i])
-        for i, (src, dst) in enumerate(((x_hbm, x_ref), (raw_hbm, raw_ref), (cot_hbm, cot_ref)))
+        for i, (src, dst) in enumerate(
+            (
+                (bin_hbm, bin_ref), (cout_hbm, cout_ref), (x_hbm, x_ref), (raw_hbm, raw_ref),
+                (cot_hbm, cot_ref), (dl_hbm, dl_ref), (bias_hbm, bias_ref), (skip_hbm, skip_ref),
+            )
+        )
     ]
     for copy in mix_in:
         copy.start()
 
+    def shifted_row(by):
+        return {"seq": lax.rem(s + (by % NROW) * ROW, NSEQ)}
+
     barrier = pltpu.get_barrier_semaphore()
-
-    @pl.loop(0, NSEQ)
-    def _(i):
-        @pl.when(i != s)
-        def _():
-            pl.semaphore_signal(barrier, inc=1, device_id={"seq": i}, device_id_type=MESH)
-
-    @pl.loop(0, NGRP)
-    def _(i):
-        @pl.when(i != g)
-        def _():
-            pl.semaphore_signal(barrier, inc=1, device_id={"grp": i}, device_id_type=MESH)
-
-    pl.semaphore_wait(barrier, NSEQ + NGRP - 2)
+    for off in range(1, ROW):
+        pl.semaphore_signal(barrier, inc=1, device_id={"seq": base + lax.rem(col + off, ROW)}, device_id_type=MESH)
+    for by in (1, -1):
+        pl.semaphore_signal(barrier, inc=1, device_id=shifted_row(by), device_id_type=MESH)
+    for off in range(1, NGRP):
+        pl.semaphore_signal(barrier, inc=1, device_id={"grp": lax.rem(g + off, NGRP)}, device_id_type=MESH)
+    pl.semaphore_wait(barrier, ROW + NGRP)
+
+    def tell_rows(step):
+        for by in ((1, -1), (2, -2), (4,))[step]:
+            pl.semaphore_signal(heard.at[step], inc=1, device_id=shifted_row(by), device_id_type=MESH)
+
+    def hear_rows(step):
+        pl.semaphore_wait(heard.at[step], (2, 2, 1)[step])
+
+    tell_rows(0)
 
     srcs = (k_hbm, v_hbm, q_hbm, do_hbm)
     dsts = (ks, vs, qs, dos)
@@ -617,10 +627,19 @@
     send((K, 0), (VV, 0))()
     for h in range(HPD):
         forward_own(h)
+    for copy in mix_in[:2]:
+        copy.wait()
     mixer_tables()
-    for copy in mix_in:
+    for copy in mix_in[2:]:
         copy.wait()
-    tiles(mixer_local, 0, TILES, [(4, send((Q, 0)))])
+    def pass_on(step):
+        hear_rows(step)
+        tell_rows(step + 1)
+
+    tiles(
+        mixer_local, 0, TILES,
+        [(4, send((Q, 0))), (6, lambda: pass_on(0)), (12, lambda: pass_on(1)), (18, lambda: hear_rows(2))],
+    )
     scatter(tot, gath, a_send, a_recv)
     scatter(dtot, gdt, t_send, t_recv)
     send((DO, 0))()
@@ -630,9 +649,9 @@
     forward_rest(0)
     send((K, 1), (VV, 1), (K, 2), (VV, 2), (Q, 1), (DO, 1), (Q, 2), (DO, 2))()
     tiles_wait(cin, b_recv)
-    tiles(mixer_back, 0, TILES // 2, [(9, lambda: forward_rest(1))])
+    tiles(mixer_back, 0, 13, [(9, lambda: forward_rest(1))])
     attention(0, [(2, lambda: forward_rest(2))])
-    tiles(mixer_back, TILES // 2, TILES, [])
+    tiles(mixer_back, 13, TILES, [])
     scatter(par, pgat, c_send, c_recv)
     mixer_state_grads()
     attention(1, [])
@@ -671,7 +690,8 @@
         V((HPD, OWN, HD), BF16), V((HPD, OWN, HD), BF16), V((HPD, 2 * OWN, HD), BF16), V((HPD, 2 * OWN, HD), BF16),
         V((HPD, 2, 2 * OWN, HD), F32), V((HPD, OWN, HD), BF16),
         V((HPD, 2, OWN, HD), BF16), V((HPD, 2, OWN, HD), BF16), V((HPD, 2, OWN, HD), BF16),
-        *[V((1, TOK, INNER), BF16)] * 3, D((3,)),
+        *[V((1, TOK, INNER), BF16)] * 3, *[V((1, NST, TOK), BF16)] * 2,
+        V((NST, INNER), F32), *[V((1, INNER), F32)] * 2, D((8,)),
         *[V((TILES, NCH * PITCH, 128), F32)] * 4,
         V((TILES, LEN, NST, NCH, 128), F32), V((TILES, NST, 128), F32),
         V((NST, LEN, NCH, 128), F32), V((NST, LEN, NCH, 128), F32), V((NCH * PITCH, 128), F32),
@@ -683,7 +703,7 @@
         V((NST, LEN * NCH, 128), F32), V((NST, LEN * NCH, 128), F32), V((NST, 128), F32),
         V((TILES, 10, 128), F32), V((NSEQ, 10, 128), F32), V((10, 128), F32), V((NGRP, 10, 128), F32),
         V((10, 128), F32), V((TILES, 10, 128), F32),
-        D((4, HPD, ROW - 1)), D((4, HPD, ROW - 1)), D((4, HPD)),
+        pltpu.SemaphoreType.REGULAR((3,)), D((4, HPD, ROW - 1)), D((4, HPD, ROW - 1)), D((4, HPD)),
         *[D((2, HPD, ROW))] * 4,
         D((3, HPD, ROW)), D((3, HPD, ROW)), D((3, HPD)),
         *[D(())] * 12,
@@ -691,7 +711,7 @@
     res = pl.pallas_call(
         kernel,
         out_shape=tuple(V(a.shape, a.dtype) for a in shapes),
-        in_specs=[hbm] * 6 + [vm] * 2 + [hbm] + [vm] * 3,
+        in_specs=[hbm] * 12,
         out_specs=(vm,) * 10,
         scratch_shapes=scratch,
         compiler_params=pltpu.CompilerParams(

time: 82.2 us -> 81.3 us (0.989)
  Pallas kernels: 80.7 us -> 79.8 us
    pallas_call x1, Pallas kernels: 78.7 us -> 77.8 us  [per_device(): pl.pallas_call(kernel, out_shape=tuple((V(a.shape, a.dtype) for a in shap...]
where the time goes in v5:
time: 81.3 us; the launch traced here: 80.4 us
  Pallas kernels  79.8 us (98%)
    pallas_call x1, Pallas kernels, per_device(): pl.pallas_call(kernel, out_shape=tuple((V(a.shape, a.dtype) for a in shap...  77.8 us
    pallas_call x1, Pallas kernels, per_device(): pl.pallas_call(store_results, out_shape=shapes, in_specs=[vm] * len(shape...  2.04 us

profile of v5, /device:TPU:30, one launch (start us, length us, event | category | flops | bytes accessed | tf_op | source)
XLA Modules:
  0.0 80.4 jit_solution(12223518400719335574)
XLA Ops:
  0.6 77.8 %shard_map.195 = (bf16[1,256,1536]{2,1,0:T(8,128)(2,1)S(1)}, bf16[1,256,1536]{2,1,0:T(8,128)(2,1)S(1)}, bf16[1,256,1536]{2,1,0:T(8,128)(2,1)S(1)}, bf16[1,128,30...) custom-call(bf16[1,256,1536]{2,1,0:T(8,128)(2,1)} %q_hbm.1, ...), custom_call_target="tpu_custom_call" | custom-call | tf_op jit(solution)/shard_map/pallas_call | solution.py:711
  78.4 2.0 %shard_map.196 = (bf16[1,256,1536]{2,1,0:T(8,128)(2,1)}, bf16[1,256,1536]{2,1,0:T(8,128)(2,1)}, bf16[1,256,1536]{2,1,0:T(8,128)(2,1)}, bf16[1,128,3072]{2,1,0:T(...) custom-call(bf16[1,256,1536]{2,1,0:T(8,128)(2,1)S(1)} %get-tuple-ele, ...), custom_call_target="tpu_custom_call" | custom-call | tf_op jit(solution)/shard_map/pallas_call | solution.py:721
